TPU v7x, 32 devices: a whole 2x2x4 slice. The times are simulated.
32 devices in a mesh: dp: 8 (over z, x), expert: 4 (over y, core).
Axes of the slice: x: 2, y: 2, z: 4, core: 2. Of those that a mesh axis runs over, the one named last changes fastest.
Arguments:
- tokens: bfloat16 [4096, 1024], P(('dp', 'expert')), may hold values from -24 to 24
- cotangent: bfloat16 [4096, 1024], P(('dp', 'expert')), may hold values from -6 to 6
- prefix: int32 [8], P('dp'), may hold values from 51 to 256
- expert_choice: int32 [4096, 1], P(('dp', 'expert')), may hold values from 0 to 3; in each aligned block of 128 rows (0 to 127, 128 to 255, ...) at most 64 rows name the same one
- norm1_gain: bfloat16 [1024], P(('dp', 'expert')), may hold values from 0.099609375 to 1.8984375
- w_qkv: bfloat16 [1024, 3072], P(('dp', 'expert')), may hold values from -0.1875 to 0.1875
- w_out: bfloat16 [1024, 1024], P(('dp', 'expert')), may hold values from -1.5 to 1.5
- norm2_gain: bfloat16 [1024], P(('dp', 'expert')), may hold values from 0.099609375 to 1.8984375
- w_up: bfloat16 [1024, 4096], P(('dp', 'expert')), may hold values from -0.1875 to 0.1875
- w_down: bfloat16 [4096, 1024], P(('dp', 'expert')), may hold values from -0.09375 to 0.09375
- w_router: bfloat16 [1024, 4], P(('dp', 'expert')), may hold values from -0.125 to 0.125
- w_mix: bfloat16 [1024, 2], P(('dp', 'expert')), may hold values from -0.1875 to 0.1875
- expert_up: bfloat16 [4096, 4, 1024], P('dp', 'expert'), may hold values from -0.1875 to 0.1875
- expert_down: bfloat16 [4096, 4, 1024], P('dp', 'expert'), may hold values from -0.375 to 0.375
Outputs:
- output: float32 [4096, 1024], P(('dp', 'expert'))
- grad_tokens: float32 [4096, 1024], P(('dp', 'expert'))
- grad_norm1_gain: float32 [1024], P(('dp', 'expert'))
- grad_w_qkv: float32 [1024, 3072], P(('dp', 'expert'))
- grad_w_out: float32 [1024, 1024], P(('dp', 'expert'))
- grad_norm2_gain: float32 [1024], P(('dp', 'expert'))
- grad_w_up: float32 [1024, 4096], P(('dp', 'expert'))
- grad_w_down: float32 [4096, 1024], P(('dp', 'expert'))
- grad_w_router: float32 [1024, 4], P(('dp', 'expert'))
- grad_w_mix: float32 [1024, 2], P(('dp', 'expert'))
- grad_expert_up: float32 [4096, 4, 1024], P('dp', 'expert')
- grad_expert_down: float32 [4096, 4, 1024], P('dp', 'expert')
- rms_mid: float32 [], replicated
- rms_attn: float32 [], replicated
- rms_ffn: float32 [], replicated
- rms_out: float32 [], replicated
Inputs may be any that keep to these rules, and one draw needn't show every extreme that they name: `expert_choice`: among the 128 rows of one device no expert is chosen more than 64 times.
All inputs are finite; a program needn't handle non-finite values.
Results may differ from a plain program's by a relative error of at most 0.033.
Values may be sent and summed in bfloat16 or wider, within the bound.
A program may use at most 192 MiB of HBM per device.

v0:
```python
import jax
import jax.numpy as jnp
from jax import lax
from jax.sharding import PartitionSpec as P

HEAD = 64


EPS = 1e-05
NEG_FILL = -1e30
HIGHEST = lax.Precision.HIGHEST
ROWS_AXIS = (((0,), (0,)), ((), ()))
COLS_AXIS = (((1,), (1,)), ((), ()))


def layer_norm(values, norm_gain):
    row_mean = jnp.mean(values, axis=-1, keepdims=True)
    centered = values - row_mean
    inverse = lax.rsqrt(jnp.mean(centered * centered, axis=-1, keepdims=True) + EPS)
    normed = centered * inverse
    return (normed * norm_gain, normed, inverse)


def norm_back(grad_out, normed, inverse, norm_gain):
    scaled = grad_out * norm_gain
    mean_one = jnp.mean(scaled, axis=-1, keepdims=True)
    mean_two = jnp.mean(scaled * normed, axis=-1, keepdims=True)
    return (inverse * (scaled - mean_one - normed * mean_two), jnp.sum(grad_out * normed, axis=0))


def gelu_tanh(values):
    return jax.nn.gelu(values, approximate=True)


def gelu_back(pre_act, grad_act):
    return jax.vjp(gelu_tanh, pre_act)[1](grad_act)[0]


def softmax_rows(logits):
    shifted = logits - jnp.max(logits, axis=-1, keepdims=True)
    weights = jnp.exp(shifted)
    return weights / jnp.sum(weights, axis=-1, keepdims=True)


def contract_rows(left_side, right_side):
    return lax.dot_general(left_side, right_side, ROWS_AXIS, preferred_element_type=jnp.float32)


def contract_cols(left_side, right_side):
    return lax.dot_general(left_side, right_side, COLS_AXIS, preferred_element_type=jnp.float32)


def precise_rows(left_side, right_side):
    return lax.dot_general(
        left_side, right_side, ROWS_AXIS, precision=HIGHEST, preferred_element_type=jnp.float32
    )


def precise_cols(left_side, right_side):
    return lax.dot_general(
        left_side, right_side, COLS_AXIS, precision=HIGHEST, preferred_element_type=jnp.float32
    )


def per_device(
    tokens,
    cotangent,
    prefix,
    expert_choice,
    norm1_gain,
    w_qkv,
    w_out,
    norm2_gain,
    w_up,
    w_down,
    w_router,
    w_mix,
    expert_up,
    expert_down,
):
    local_rows, model_width = tokens.shape
    experts = lax.axis_size("expert")
    replicas = lax.axis_size("dp")
    capacity = 2 * local_rows // experts
    cut_width = model_width // experts
    head_count = cut_width // HEAD
    ff_cut = w_up.shape[1] // experts
    row_share = w_qkv.shape[0]
    ff_share = w_down.shape[0]
    stride = replicas // experts
    my_block = lax.axis_index("dp") * experts + lax.axis_index("expert")
    score_scale = HEAD ** (-0.5)

    def fetch_weights():
        small = (
            lax.all_gather(norm1_gain, ("dp", "expert"), axis=0, tiled=True),
            lax.all_gather(norm2_gain, ("dp", "expert"), axis=0, tiled=True),
            lax.all_gather(w_router, ("dp", "expert"), axis=0, tiled=True),
            lax.all_gather(w_mix, ("dp", "expert"), axis=0, tiled=True),
        )
        big = (
            lax.all_gather(w_qkv, "dp", axis=0, tiled=True),
            lax.all_gather(w_up, "dp", axis=0, tiled=True),
            lax.all_gather(w_out, "dp", axis=0, tiled=True),
            lax.all_gather(w_down, "dp", axis=0, tiled=True),
            lax.all_gather(expert_up, "dp", axis=0, tiled=True),
            lax.all_gather(expert_down, "dp", axis=0, tiled=True),
        )
        qkv_rows, up_rows, out_rows, down_rows, expert_in_full, expert_out_full = big
        span = qkv_rows.shape[0]
        outgoing = (
            jnp.moveaxis(qkv_rows.reshape(span, 3, experts, cut_width), 2, 0),
            jnp.moveaxis(up_rows.reshape(span, experts, ff_cut), 1, 0),
            out_rows.reshape(experts, stride * row_share, model_width),
            down_rows.reshape(experts, stride * ff_share, model_width),
        )
        qkv_in, up_in, out_in, down_in = (
            lax.all_to_all(outgoing[0], "expert", split_axis=0, concat_axis=0, tiled=True),
            lax.all_to_all(outgoing[1], "expert", split_axis=0, concat_axis=0, tiled=True),
            lax.all_to_all(outgoing[2], "expert", split_axis=0, concat_axis=0, tiled=True),
            lax.all_to_all(outgoing[3], "expert", split_axis=0, concat_axis=0, tiled=True),
        )
        qkv_w = jnp.transpose(
            qkv_in.reshape(experts, replicas, row_share, 3 * cut_width), (1, 0, 2, 3)
        ).reshape(model_width, 3 * cut_width)
        up_w = jnp.transpose(
            up_in.reshape(experts, replicas, row_share, ff_cut), (1, 0, 2, 3)
        ).reshape(model_width, ff_cut)
        out_w = jnp.transpose(
            out_in.reshape(experts, stride, row_share, model_width), (1, 0, 2, 3)
        ).reshape(cut_width, model_width)
        down_w = jnp.transpose(
            down_in.reshape(experts, stride, ff_share, model_width), (1, 0, 2, 3)
        ).reshape(ff_cut, model_width)
        return (
            small[0].astype(jnp.float32),
            small[1].astype(jnp.float32),
            small[2],
            small[3],
            qkv_w,
            up_w,
            out_w,
            down_w,
            expert_in_full[:, 0, :],
            expert_out_full[:, 0, :],
        )

    def spread(rows_low):
        return lax.all_gather(rows_low, "expert", axis=0, tiled=True)

    def fold(term_fn):
        return lax.psum_scatter(
            term_fn(jnp.int32(0), lax.axis_size("expert") * local_rows).astype(jnp.bfloat16),
            "expert",
            scatter_dimension=0,
            tiled=True,
        ).astype(jnp.float32)

    weights = fetch_weights()
    gain_one, gain_two, router_w, mix_w, qkv_w, up_w, out_w, down_w, expert_in_w, expert_out_w = (
        weights
    )
    inputs = tokens.astype(jnp.float32)
    scaled_one, normed_one, inverse_one = layer_norm(inputs, gain_one)
    normed_low = scaled_one.astype(jnp.bfloat16)
    normed_all = spread(normed_low)
    seq_len = normed_all.shape[0]
    qkv_cut = jnp.dot(normed_all, qkv_w, preferred_element_type=jnp.float32).astype(jnp.bfloat16)
    queries = qkv_cut[:, :cut_width].reshape(seq_len, head_count, HEAD)
    keys = qkv_cut[:, cut_width : 2 * cut_width].reshape(seq_len, head_count, HEAD)
    values = qkv_cut[:, 2 * cut_width :].reshape(seq_len, head_count, HEAD)
    query_block = min(512, seq_len)
    block_count = seq_len // query_block
    key_pos = jnp.arange(seq_len, dtype=jnp.int32)
    prefix_len = prefix[0]

    def block_scores(first_row, query_part):
        query_pos = first_row + jnp.arange(query_block, dtype=jnp.int32)
        visible = (key_pos[None, :] <= query_pos[:, None]) | (key_pos[None, :] < prefix_len)
        scores = (
            jnp.einsum("qhd,khd->hqk", query_part, keys, preferred_element_type=jnp.float32)
            * score_scale
        )
        return jnp.where(visible[None], scores, NEG_FILL)

    def forward_block(block_index):
        first_row = block_index * query_block
        query_part = lax.dynamic_slice_in_dim(queries, first_row, query_block, 0)
        masked = block_scores(first_row, query_part)
        row_max = jnp.max(masked, axis=-1, keepdims=True)
        expd = jnp.exp(masked - row_max)
        row_total = jnp.sum(expd, axis=-1, keepdims=True)
        weights_low = (expd / row_total).astype(jnp.bfloat16)
        mixed_out = jnp.einsum(
            "hqk,khd->qhd", weights_low, values, preferred_element_type=jnp.float32
        )
        return (mixed_out.reshape(query_block, cut_width), (row_max + jnp.log(row_total))[..., 0])

    mixed_blocks, row_lse = lax.map(forward_block, jnp.arange(block_count))
    attended_cut = mixed_blocks.reshape(seq_len, cut_width).astype(jnp.bfloat16)

    def attn_term(first_row, row_count):
        return jnp.dot(attended_cut, out_w, preferred_element_type=jnp.float32)

    attn_out = fold(attn_term)
    middle = inputs + attn_out
    scaled_two, normed_two, inverse_two = layer_norm(middle, gain_two)
    hidden_low = scaled_two.astype(jnp.bfloat16)
    router_probs = softmax_rows(jnp.dot(hidden_low, router_w, preferred_element_type=jnp.float32))
    chosen = expert_choice[:, 0]
    onehot_int = (jnp.arange(experts, dtype=jnp.int32)[None, :] == chosen[:, None]).astype(
        jnp.int32
    )
    onehot = onehot_int.astype(jnp.float32)
    gate_prob = jnp.sum(router_probs * onehot, axis=-1)
    mix_coef = softmax_rows(jnp.dot(hidden_low, mix_w, preferred_element_type=jnp.float32))
    hidden_all = spread(hidden_low)
    dense_pre = jnp.dot(hidden_all, up_w, preferred_element_type=jnp.float32)
    dense_act = gelu_tanh(dense_pre).astype(jnp.bfloat16)

    def dense_term(first_row, row_count):
        return jnp.dot(dense_act, down_w, preferred_element_type=jnp.float32)

    dense_out = fold(dense_term)
    earlier = jnp.cumsum(onehot_int, axis=0) - onehot_int
    slot_index = chosen * capacity + jnp.sum(earlier * onehot_int, axis=-1)
    send_rows = (
        jnp.zeros((experts * capacity, model_width), jnp.bfloat16).at[slot_index].set(hidden_low)
    )
    received = lax.all_to_all(
        send_rows.reshape(experts, capacity, model_width),
        "expert",
        split_axis=0,
        concat_axis=0,
        tiled=True,
    )
    pre_act = jnp.einsum("ncd,fd->ncf", received, expert_in_w, preferred_element_type=jnp.float32)
    act_low = gelu_tanh(pre_act).astype(jnp.bfloat16)
    out_low = jnp.einsum(
        "ncf,fd->ncd", act_low, expert_out_w, preferred_element_type=jnp.float32
    ).astype(jnp.bfloat16)
    returned = lax.all_to_all(out_low, "expert", split_axis=0, concat_axis=0, tiled=True)
    expert_rows = returned.reshape(experts * capacity, model_width)[slot_index].astype(jnp.float32)
    coef_dense = mix_coef[:, 0:1]
    coef_expert = (mix_coef[:, 1] * gate_prob)[:, None]
    ffn_out = coef_dense * dense_out + coef_expert * expert_rows
    result = middle + ffn_out
    square_stats = jnp.stack(
        [
            jnp.sum(middle * middle),
            jnp.sum(attn_out * attn_out),
            jnp.sum(ffn_out * ffn_out),
            jnp.sum(result * result),
        ]
    )
    weights = fetch_weights()
    gain_one, gain_two, router_w, mix_w, qkv_w, up_w, out_w, down_w, expert_in_w, expert_out_w = (
        weights
    )
    grad_out = cotangent.astype(jnp.float32)
    grad_dense = (grad_out * coef_dense).astype(jnp.bfloat16)
    grad_expert = (grad_out * coef_expert).astype(jnp.bfloat16)
    dense_dot = jnp.sum(grad_out * dense_out, axis=-1)
    expert_dot = jnp.sum(grad_out * expert_rows, axis=-1)
    coef_grad = jnp.stack([dense_dot, expert_dot * gate_prob], axis=-1)
    grad_mix = mix_coef * (coef_grad - jnp.sum(mix_coef * coef_grad, axis=-1, keepdims=True))
    gate_grad = expert_dot * mix_coef[:, 1]
    grad_router = (gate_grad * gate_prob)[:, None] * (onehot - router_probs)
    grad_send = (
        jnp.zeros((experts * capacity, model_width), jnp.bfloat16).at[slot_index].set(grad_expert)
    )
    grad_received = lax.all_to_all(
        grad_send.reshape(experts, capacity, model_width),
        "expert",
        split_axis=0,
        concat_axis=0,
        tiled=True,
    )
    grad_act_e = jnp.einsum(
        "ncd,fd->ncf", grad_received, expert_out_w, preferred_element_type=jnp.float32
    )
    grad_pre_e = gelu_back(pre_act, grad_act_e).astype(jnp.bfloat16)
    grad_in_e = jnp.einsum(
        "ncf,fd->ncd", grad_pre_e, expert_in_w, preferred_element_type=jnp.float32
    ).astype(jnp.bfloat16)
    grad_returned = lax.all_to_all(grad_in_e, "expert", split_axis=0, concat_axis=0, tiled=True)
    grad_hidden_expert = grad_returned.reshape(experts * capacity, model_width)[slot_index].astype(
        jnp.float32
    )
    slot_rows = experts * capacity
    expert_up_term = contract_rows(
        grad_pre_e.reshape(slot_rows, -1), received.reshape(slot_rows, model_width)
    )
    expert_down_term = contract_rows(
        act_low.reshape(slot_rows, -1), grad_received.reshape(slot_rows, model_width)
    )
    grad_dense_all = spread(grad_dense)
    grad_w_down_cut = contract_rows(dense_act, grad_dense_all)
    grad_act_d = contract_cols(grad_dense_all, down_w)
    grad_pre_d = gelu_back(dense_pre, grad_act_d).astype(jnp.bfloat16)
    grad_w_up_cut = contract_rows(hidden_all, grad_pre_d)

    def hidden_term(first_row, row_count):
        return contract_cols(grad_pre_d, up_w)

    hidden_wide = hidden_low.astype(jnp.float32)
    grad_hidden = fold(hidden_term) + grad_hidden_expert
    grad_hidden = (
        grad_hidden
        + precise_cols(grad_router, router_w.astype(jnp.float32))
        + precise_cols(grad_mix, mix_w.astype(jnp.float32))
    )
    grad_w_router = precise_rows(hidden_wide, grad_router)
    grad_w_mix = precise_rows(hidden_wide, grad_mix)
    grad_mid_norm, grad_gain_two = norm_back(grad_hidden, normed_two, inverse_two, gain_two)
    grad_middle = grad_out + grad_mid_norm
    grad_attn = grad_middle.astype(jnp.bfloat16)
    grad_attn_all = spread(grad_attn)
    grad_w_out_cut = contract_rows(attended_cut, grad_attn_all)
    grad_att_cut = contract_cols(grad_attn_all, out_w).astype(jnp.bfloat16)

    def backward_block(carry, block_index):
        key_sum, value_sum = carry
        first_row = block_index * query_block
        query_part = lax.dynamic_slice_in_dim(queries, first_row, query_block, 0)
        grad_part = lax.dynamic_slice_in_dim(grad_att_cut, first_row, query_block, 0).reshape(
            query_block, head_count, HEAD
        )
        masked = block_scores(first_row, query_part)
        prob_rows = jnp.exp(masked - row_lse[block_index][:, :, None])
        grad_probs = jnp.einsum(
            "qhd,khd->hqk", grad_part, values, preferred_element_type=jnp.float32
        )
        row_delta = jnp.sum(prob_rows * grad_probs, axis=-1, keepdims=True)
        grad_scores = (prob_rows * (grad_probs - row_delta)).astype(jnp.bfloat16)
        grad_query = (
            jnp.einsum("hqk,khd->qhd", grad_scores, keys, preferred_element_type=jnp.float32)
            * score_scale
        )
        key_sum = (
            key_sum
            + jnp.einsum(
                "hqk,qhd->khd", grad_scores, query_part, preferred_element_type=jnp.float32
            )
            * score_scale
        )
        value_sum = value_sum + jnp.einsum(
            "hqk,qhd->khd",
            prob_rows.astype(jnp.bfloat16),
            grad_part,
            preferred_element_type=jnp.float32,
        )
        return ((key_sum, value_sum), grad_query.reshape(query_block, cut_width))

    empty_heads = jnp.zeros((seq_len, head_count, HEAD), jnp.float32)
    (key_sum, value_sum), query_blocks = lax.scan(
        backward_block, (empty_heads, empty_heads), jnp.arange(block_count)
    )
    grad_qkv_cut = jnp.concatenate(
        [
            query_blocks.reshape(seq_len, cut_width),
            key_sum.reshape(seq_len, cut_width),
            value_sum.reshape(seq_len, cut_width),
        ],
        axis=1,
    ).astype(jnp.bfloat16)
    grad_w_qkv_cut = contract_rows(normed_all, grad_qkv_cut)

    def normed_term(first_row, row_count):
        return contract_cols(grad_qkv_cut, qkv_w)

    grad_normed = fold(normed_term)
    grad_in_norm, grad_gain_one = norm_back(grad_normed, normed_one, inverse_one, gain_one)
    grad_tokens = grad_middle + grad_in_norm
    send_grads = (
        jnp.moveaxis(grad_w_qkv_cut.reshape(replicas, experts, row_share, 3 * cut_width), 1, 0),
        jnp.moveaxis(grad_w_up_cut.reshape(replicas, experts, row_share, ff_cut), 1, 0),
        jnp.transpose(
            grad_w_out_cut.reshape(stride, experts, row_share, model_width), (1, 0, 2, 3)
        ),
        jnp.transpose(
            grad_w_down_cut.reshape(stride, experts, ff_share, model_width), (1, 0, 2, 3)
        ),
    )
    qkv_back, up_back, out_back, down_back = (
        lax.all_to_all(
            send_grads[0].astype(jnp.bfloat16), "expert", split_axis=0, concat_axis=0, tiled=True
        ).astype(jnp.float32),
        lax.all_to_all(
            send_grads[1].astype(jnp.bfloat16), "expert", split_axis=0, concat_axis=0, tiled=True
        ).astype(jnp.float32),
        lax.all_to_all(
            send_grads[2].astype(jnp.bfloat16), "expert", split_axis=0, concat_axis=0, tiled=True
        ).astype(jnp.float32),
        lax.all_to_all(
            send_grads[3].astype(jnp.bfloat16), "expert", split_axis=0, concat_axis=0, tiled=True
        ).astype(jnp.float32),
    )
    qkv_grad_rows = jnp.transpose(
        qkv_back.reshape(experts, replicas, row_share, 3, cut_width), (1, 2, 3, 0, 4)
    ).reshape(replicas * row_share, 3 * model_width)
    up_grad_rows = jnp.transpose(up_back, (1, 2, 0, 3)).reshape(
        replicas * row_share, experts * ff_cut
    )
    out_grad_rows = out_back.reshape(replicas * row_share, model_width)
    down_grad_rows = down_back.reshape(replicas * ff_share, model_width)
    summed = (
        lax.psum_scatter(
            qkv_grad_rows.astype(jnp.bfloat16), "dp", scatter_dimension=0, tiled=True
        ).astype(jnp.float32),
        lax.psum_scatter(
            up_grad_rows.astype(jnp.bfloat16), "dp", scatter_dimension=0, tiled=True
        ).astype(jnp.float32),
        lax.psum_scatter(
            out_grad_rows.astype(jnp.bfloat16), "dp", scatter_dimension=0, tiled=True
        ).astype(jnp.float32),
        lax.psum_scatter(
            down_grad_rows.astype(jnp.bfloat16), "dp", scatter_dimension=0, tiled=True
        ).astype(jnp.float32),
        lax.psum_scatter(
            expert_up_term[:, None, :].astype(jnp.bfloat16), "dp", scatter_dimension=0, tiled=True
        ).astype(jnp.float32),
        lax.psum_scatter(
            expert_down_term[:, None, :].astype(jnp.bfloat16), "dp", scatter_dimension=0, tiled=True
        ).astype(jnp.float32),
    )
    totals = lax.psum(
        (square_stats, grad_gain_one, grad_gain_two, grad_w_router, grad_w_mix), ("dp", "expert")
    )
    first_row = my_block * row_share
    own_gain_one = lax.dynamic_slice_in_dim(totals[1], first_row, row_share, 0)
    own_gain_two = lax.dynamic_slice_in_dim(totals[2], first_row, row_share, 0)
    own_router = lax.dynamic_slice_in_dim(totals[3], first_row, row_share, 0)
    own_mix = lax.dynamic_slice_in_dim(totals[4], first_row, row_share, 0)
    entry_count = local_rows * model_width * replicas * experts
    rms_values = jnp.sqrt(totals[0] / entry_count + 1e-06)
    return (
        result,
        grad_tokens,
        own_gain_one,
        summed[0],
        summed[2],
        own_gain_two,
        summed[1],
        summed[3],
        own_router,
        own_mix,
        summed[4],
        summed[5],
        rms_values[0],
        rms_values[1],
        rms_values[2],
        rms_values[3],
    )


def solution(mesh):
    return jax.shard_map(
        per_device,
        mesh=mesh,
        in_specs=(
            P(("dp", "expert"), None),
            P(("dp", "expert"), None),
            P("dp"),
            P(("dp", "expert"), None),
            P(("dp", "expert")),
            P(("dp", "expert"), None),
            P(("dp", "expert"), None),
            P(("dp", "expert")),
            P(("dp", "expert"), None),
            P(("dp", "expert"), None),
            P(("dp", "expert"), None),
            P(("dp", "expert"), None),
            P("dp", "expert", None),
            P("dp", "expert", None),
        ),
        out_specs=(
            P(("dp", "expert"), None),
            P(("dp", "expert"), None),
            P(("dp", "expert")),
            P(("dp", "expert"), None),
            P(("dp", "expert"), None),
            P(("dp", "expert")),
            P(("dp", "expert"), None),
            P(("dp", "expert"), None),
            P(("dp", "expert"), None),
            P(("dp", "expert"), None),
            P("dp", "expert", None),
            P("dp", "expert", None),
            P(),
            P(),
            P(),
            P(),
        ),
        check_vma=False,
    )
```

profile of v0, /device:TPU:0, one launch (start us, length us, event | category | flops | bytes accessed | tf_op | source)
XLA Modules:
  0.0 1283.8 jit_solution(16454437754500315036)
XLA Ops:
  7.9 35.7 %all_gather.55 = bf16[256,1024]{1,0:T(8,128)(2,1)} all-gather(bf16[32,1024]{1,0:T(8,128)(2,1)} %param.20), channel_id=1, replica_groups=mesh['dp'=8,'expert'=4] {'dp'}, dimensions={0}, use_global_device_ids=true | all-gather | bytes 589824 | tf_op jit(solution)/shard_map/all_gather | solution.py:104
  48.9 41.7 %all-reduce.3 = (bf16[1024]{0:T(1024)(128)(2,1)S(1)}, bf16[1024]{0:T(1024)(128)(2,1)S(1)}) all-reduce(bf16[1024]{0:T(1024)(128)(2,1)S(1)} %dynamic-update-slice.1, bf16[1024]{0:T(1024)(128)(2,1)S(1)} %dynamic-update-slice), channel_id=1, replica_groups=mesh['dp'=8,'expert'=4] {'dp','expert'}, use_global_device_ids=true, to_apply=%add.1 | all-reduce | flops 2048 | bytes 8192
  101.5 23.0 %all-to-all-done = bf16[4,256,3,256]{3,1,2,0:T(8,128)(2,1)} async-done(((bf16[4,256,3,256]{3,1,2,0:T(8,128)(2,1)}), bf16[4,256,3,256]{3,1,2,0:T(8,128)(2,1)}, u32[]{:S(2)}, u32[]{:S(2)}) %all-to-all-start) | async-done | bytes 1572896 | tf_op jit(solution)/shard_map/all_to_all | solution.py:118
  143.1 23.7 %reduce-scatter.11.cloned.1.call-done = bf16[128,1024]{1,0:T(8,128)(2,1)} async-done(((bf16[512,1024]{1,0:T(8,128)(2,1)}), bf16[128,1024]{1,0:T(8,128)(2,1)}) %reduce-scatter.11.cloned.1.call-update) | async-done | bytes 262160 | tf_op jit(solution)/shard_map/reduce_scatter | solution.py:152
  172.4 45.5 %all-gather.20.cloned.1.call-done = bf16[1024,1024]{1,0:T(8,128)(2,1)} async-done(((bf16[128,1024]{1,0:T(8,128)(2,1)}), bf16[1024,1024]{1,0:T(8,128)(2,1)}) %all-gather.20.cloned.1.call-update) | async-done | bytes 2097168 | tf_op jit(solution)/shard_map/all_gather | solution.py:105
  221.5 46.0 %all-gather.18.cloned.1.call-done = bf16[256,4096]{1,0:T(8,128)(2,1)} async-done(((bf16[32,4096]{1,0:T(8,128)(2,1)}), bf16[256,4096]{1,0:T(8,128)(2,1)}) %all-gather.18.cloned.1.call-update) | async-done | bytes 2097168 | tf_op jit(solution)/shard_map/all_gather | solution.py:103
  276.2 62.8 %all-gather = bf16[32,32,2]{1,2,0:T(2,128)(2,1)S(1)} all-gather(bf16[1,32,2]{1,2,0:T(2,128)(2,1)S(1)} %bitcast.245), channel_id=1, replica_groups=mesh['dp'=8,'expert'=4] {'dp','expert'}, dimensions={0}, use_global_device_ids=true | all-gather | bytes 4224 | tf_op jit(solution)/shard_map/all_gather | solution.py:99
  339.2 38.3 %all-gather.1 = bf16[32,32,4]{1,2,0:T(4,128)(2,1)S(1)} all-gather(bf16[1,32,4]{1,2,0:T(4,128)(2,1)S(1)} %bitcast.244), channel_id=1, replica_groups=mesh['dp'=8,'expert'=4] {'dp','expert'}, dimensions={0}, use_global_device_ids=true | all-gather | bytes 8448 | tf_op jit(solution)/shard_map/all_gather | solution.py:98
  398.4 18.9 %all-gather.22.cloned.1.call-done = bf16[4096,1,1024]{2,0,1:T(8,128)(2,1)} async-done(((bf16[512,1,1024]{2,0,1:T(8,128)(2,1)}), bf16[4096,1,1024]{2,0,1:T(8,128)(2,1)}) %all-gather.22.cloned.1.call-update) | async-done | bytes 8388624 | tf_op jit(solution)/shard_map/all_gather | solution.py:106
  425.0 117.2 %all-gather.24.cloned.1.call-done = bf16[4096,1,1024]{2,0,1:T(8,128)(2,1)} async-done(((bf16[512,1,1024]{2,0,1:T(8,128)(2,1)}), bf16[4096,1,1024]{2,0,1:T(8,128)(2,1)}) %all-gather.24.cloned.1.call-update) | async-done | bytes 8388624 | tf_op jit(solution)/shard_map/all_gather | solution.py:107
  554.0 11.0 all-to-all-done.5
  578.3 14.4 %all-gather.26.cloned.1.call-done = bf16[512,1024]{1,0:T(8,128)(2,1)} async-done(((bf16[128,1024]{1,0:T(8,128)(2,1)}), bf16[512,1024]{1,0:T(8,128)(2,1)}) %all-gather.26.cloned.1.call-update) | async-done | bytes 1048592 | tf_op jit(solution)/shard_map/all_gather | solution.py:149
  601.1 11.4 fusion.16
  619.1 11.2 all_to_all.64
  635.1 16.3 %all-gather.28.cloned.1.call-done = bf16[512,1024]{1,0:T(8,128)(2,1)} async-done(((bf16[128,1024]{1,0:T(8,128)(2,1)}), bf16[512,1024]{1,0:T(8,128)(2,1)}) %all-gather.28.cloned.1.call-update) | async-done | bytes 1048592 | tf_op jit(solution)/shard_map/all_gather | solution.py:149
  676.2 28.1 %all_to_all.65 = bf16[4,8,32,1024]{3,2,1,0:T(8,128)(2,1)S(1)} all-to-all(bf16[4,8,32,1024]{3,2,1,0:T(8,128)(2,1)S(1)} %bitcast.200), channel_id=1, replica_groups=mesh['dp'=8,'expert'=4] {'expert'}, dimensions={0} | all-to-all | bytes 4194304 | tf_op jit(solution)/shard_map/all_to_all | solution.py:389
  711.7 28.9 %all_to_all.66 = bf16[4,2,128,1024]{3,2,1,0:T(8,128)(2,1)} all-to-all(bf16[4,2,128,1024]{3,2,1,0:T(8,128)(2,1)S(1)} %bitcast.203), channel_id=1, replica_groups=mesh['dp'=8,'expert'=4] {'expert'}, dimensions={0} | all-to-all | bytes 4194304 | tf_op jit(solution)/shard_map/all_to_all | solution.py:395
  744.0 27.9 %all_to_all.67 = bf16[4,8,32,768]{3,2,1,0:T(8,128)(2,1)} all-to-all(bf16[4,8,32,768]{3,2,1,0:T(8,128)(2,1)S(1)} %bitcast.206), channel_id=1, replica_groups=mesh['dp'=8,'expert'=4] {'expert'}, dimensions={0} | all-to-all | bytes 3145728 | tf_op jit(solution)/shard_map/all_to_all | solution.py:386
  783.5 8.4 fusion.9
  805.1 40.9 %all-reduce.2 = (f32[1024]{0:T(1024)S(1)}, f32[1024]{0:T(1024)S(1)}, f32[1024,4]{0,1:T(4,128)S(1)}, f32[1024,2]{0,1:T(2,128)S(1)}, f32[4]{0:T(128)S(1)}) all-reduce(f32[1024]{0:T(1024)S(1)} %get-tuple-element.188, f32[1024]{0:T(1024)S(1)} %get-tuple-element.185, ...), channel_id=1, replica_groups=mesh['dp'=8,'expert'=4] {'dp','expert'}, use_global_device_ids=true, to_apply=%region_28.29 | all-reduce | flops 8196 | bytes 65568 | tf_op jit(solution)/shard_map/psum | solution.py:427
  852.9 51.7 %reduce-scatter.25.cloned.1.call-done = bf16[128,1024]{1,0:T(8,128)(2,1)} async-done(((bf16[1024,1024]{1,0:T(8,128)(2,1)}), bf16[128,1024]{1,0:T(8,128)(2,1)}) %reduce-scatter.25.cloned.1.call-update) | async-done | bytes 262160 | tf_op jit(solution)/shard_map/reduce_scatter | solution.py:417
  906.4 66.2 %reduce-scatter.19.cloned.1.call-done = bf16[32,3072]{1,0:T(8,128)(2,1)} async-done(((bf16[256,3072]{1,0:T(8,128)(2,1)}), bf16[32,3072]{1,0:T(8,128)(2,1)}) %reduce-scatter.19.cloned.1.call-update) | async-done | bytes 196624 | tf_op jit(solution)/shard_map/reduce_scatter | solution.py:408
  974.3 148.1 %reduce-scatter.29.cloned.1.call-done = bf16[512,1,1024]{2,0,1:T(8,128)(2,1)} async-done(((bf16[4096,1,1024]{2,0,1:T(8,128)(2,1)}), bf16[512,1,1024]{2,0,1:T(8,128)(2,1)}) %reduce-scatter.29.cloned.1.call-update) | async-done | bytes 1048592 | tf_op jit(solution)/shard_map/reduce_scatter | solution.py:423
  1126.6 146.1 %reduce-scatter.27.cloned.1.call-done = bf16[512,1,1024]{2,0,1:T(8,128)(2,1)} async-done(((bf16[4096,1,1024]{2,0,1:T(8,128)(2,1)}), bf16[512,1,1024]{2,0,1:T(8,128)(2,1)}) %reduce-scatter.27.cloned.1.call-update) | async-done | bytes 1048592 | tf_op jit(solution)/shard_map/reduce_scatter | solution.py:420
  (244 shorter events, 204.2 us)
Async XLA Ops:
  7.2 85.7 %all-gather.14.cloned.1.call-start = ((), (), s32[]{:S(2)}) async-start(), calls=%async_computation.23 | async-start | bytes 1769472 | tf_op jit(solution)/shard_map/all_gather | solution.py:102
  43.7 52.6 %all-to-all-start.1 = ((bf16[4,64,1024]{2,1,0:T(8,128)(2,1)}), bf16[4,64,1024]{2,1,0:T(8,128)(2,1)S(1)}, u32[]{:S(2)}, u32[]{:S(2)}) async-start(bf16[4,64,1024]{2,1,0:T(8,128)(2,1)} %bitcast.10), calls=%async_computation.1 | async-start | bytes 1048576 | tf_op jit(solution)/shard_map/all_to_all | solution.py:120
  47.1 84.5 %all-gather.12.cloned.1.call-start = ((), (), s32[]{:S(2)}) async-start(), calls=%async_computation.22 | async-start | bytes 1310720 | tf_op jit(solution)/shard_map/all_gather | solution.py:149
  96.2 28.3 %all-to-all-start = ((bf16[4,256,3,256]{3,1,2,0:T(8,128)(2,1)}), bf16[4,256,3,256]{3,1,2,0:T(8,128)(2,1)}, u32[]{:S(2)}, u32[]{:S(2)}) async-start(bf16[4,256,3,256]{3,1,2,0:T(8,128)(2,1)} %copy.168), calls=%async_computation | async-start | bytes 3145728 | tf_op jit(solution)/shard_map/all_to_all | solution.py:118
  100.6 66.2 %reduce-scatter.11.cloned.1.call-start = ((), (), s32[]{:S(2)}) async-start(), calls=%async_computation.24 | async-start | bytes 1310720 | tf_op jit(solution)/shard_map/reduce_scatter | solution.py:152
  141.9 76.0 %all-gather.20.cloned.1.call-start = ((), (), s32[]{:S(2)}) async-start(), calls=%async_computation.27 | async-start | bytes 2359296 | tf_op jit(solution)/shard_map/all_gather | solution.py:105
  142.4 125.1 %all-gather.18.cloned.1.call-start = ((), (), s32[]{:S(2)}) async-start(), calls=%async_computation.26 | async-start | bytes 2359296 | tf_op jit(solution)/shard_map/all_gather | solution.py:103
  143.0 247.2 %all-gather.16.cloned.1.call-start = ((), (), s32[]{:S(2)}) async-start(), calls=%async_computation.25 | async-start | bytes 1310720 | tf_op jit(solution)/shard_map/all_gather | solution.py:149
  170.9 246.4 %all-gather.22.cloned.1.call-start = ((), (), s32[]{:S(2)}) async-start(), calls=%async_computation.29 | async-start | bytes 9437184 | tf_op jit(solution)/shard_map/all_gather | solution.py:106
  171.6 370.5 %all-gather.24.cloned.1.call-start = ((), (), s32[]{:S(2)}) async-start(), calls=%async_computation.30 | async-start | bytes 9437184 | tf_op jit(solution)/shard_map/all_gather | solution.py:107
  217.9 53.7 %all-to-all-start.3 = ((bf16[4,256,1024]{2,1,0:T(8,128)(2,1)}), bf16[4,256,1024]{2,1,0:T(8,128)(2,1)S(1)}, u32[]{:S(2)}, u32[]{:S(2)}) async-start(bf16[4,256,1024]{2,1,0:T(8,128)(2,1)} %bitcast.217), calls=%async_computation.4 | async-start | bytes 4194304 | tf_op jit(solution)/shard_map/all_to_all | solution.py:121
  271.6 108.0 %all-to-all-start.2 = ((bf16[4,256,1024]{1,2,0:T(8,128)(2,1)}), bf16[4,256,1024]{1,2,0:T(8,128)(2,1)}, u32[]{:S(2)}, u32[]{:S(2)}) async-start(bf16[4,256,1024]{1,2,0:T(8,128)(2,1)} %bitcast.198), calls=%async_computation.3 | async-start | bytes 4194304 | tf_op jit(solution)/shard_map/all_to_all | solution.py:119
  389.6 179.8 %reduce-scatter.13.cloned.1.call-start = ((), (), s32[]{:S(2)}) async-start(), calls=%async_computation.28 | async-start | bytes 1310720 | tf_op jit(solution)/shard_map/reduce_scatter | solution.py:152
  554.0 38.8 %all-gather.26.cloned.1.call-start = ((), (), s32[]{:S(2)}) async-start(), calls=%async_computation.31 | async-start | bytes 1310720 | tf_op jit(solution)/shard_map/all_gather | solution.py:149
  574.4 26.7 %all-to-all-start.6 = ((bf16[4,64,1024]{2,1,0:T(8,128)(2,1)}), bf16[4,64,1024]{2,1,0:T(8,128)(2,1)S(1)}, u32[]{:S(2)}, u32[]{:S(2)}) async-start(bf16[4,64,1024]{2,1,0:T(8,128)(2,1)} %bitcast.37), calls=%async_computation.9 | async-start | bytes 1048576 | tf_op jit(solution)/shard_map/all_to_all | solution.py:272
  577.8 53.3 %reduce-scatter.15.cloned.1.call-start = ((), (), s32[]{:S(2)}) async-start(), calls=%async_computation.32 | async-start | bytes 1310720 | tf_op jit(solution)/shard_map/reduce_scatter | solution.py:152
  601.0 50.3 %all-gather.28.cloned.1.call-start = ((), (), s32[]{:S(2)}) async-start(), calls=%async_computation.33 | async-start | bytes 1310720 | tf_op jit(solution)/shard_map/all_gather | solution.py:149
  658.2 144.2 %reduce-scatter.21.cloned.1.call-start = ((), (), s32[]{:S(2)}) async-start(), calls=%async_computation.36 | async-start | bytes 589824 | tf_op jit(solution)/shard_map/reduce_scatter | solution.py:414
  667.1 136.8 %reduce-scatter.17.cloned.1.call-start = ((), (), s32[]{:S(2)}) async-start(), calls=%async_computation.34 | async-start | bytes 1310720 | tf_op jit(solution)/shard_map/reduce_scatter | solution.py:152
  673.1 178.1 %reduce-scatter.23.cloned.1.call-start = ((), (), s32[]{:S(2)}) async-start(), calls=%async_computation.37 | async-start | bytes 2359296 | tf_op jit(solution)/shard_map/reduce_scatter | solution.py:411
  708.1 196.5 %reduce-scatter.25.cloned.1.call-start = ((), (), s32[]{:S(2)}) async-start(), calls=%async_computation.38 | async-start | bytes 2359296 | tf_op jit(solution)/shard_map/reduce_scatter | solution.py:417
  740.6 231.9 %reduce-scatter.19.cloned.1.call-start = ((), (), s32[]{:S(2)}) async-start(), calls=%async_computation.35 | async-start | bytes 1769472 | tf_op jit(solution)/shard_map/reduce_scatter | solution.py:408
  783.5 338.9 %reduce-scatter.29.cloned.1.call-start = ((), (), s32[]{:S(2)}) async-start(), calls=%async_computation.40 | async-start | bytes 9437184 | tf_op jit(solution)/shard_map/reduce_scatter | solution.py:423
  792.0 480.6 %reduce-scatter.27.cloned.1.call-start = ((), (), s32[]{:S(2)}) async-start(), calls=%async_computation.39 | async-start | bytes 9437184 | tf_op jit(solution)/shard_map/reduce_scatter | solution.py:420
  (38 other events, 574.1 us)
Sparse Core Ops, SparseCore 0:
  10.2 47.9 all-gather.13
  93.0 19.6 all-gather.11
  142.0 24.7 reduce-scatter.10
  168.8 49.0 all-gather.19
  219.9 47.6 all-gather.17
  269.5 19.2 all-gather.15
  290.9 126.3 all-gather.21
  419.4 122.6 all-gather.23
  544.7 24.7 reduce-scatter.12
  572.5 20.2 all-gather.25
  601.2 24.0 reduce-scatter.14
  635.2 16.1 all-gather.27
  667.2 62.5 reduce-scatter.20
  732.2 28.5 reduce-scatter.16
  764.8 68.9 reduce-scatter.22
  837.1 67.4 reduce-scatter.24
  907.9 64.6 reduce-scatter.18
  976.1 146.2 reduce-scatter.28
  1126.0 146.5 reduce-scatter.26
where the time goes:
time: 1290 us; the launch traced here: 1280 us
  waiting for transfers between devices  740 us (57%)
  blocking collectives  316 us (24%)
  matrix products  89.2 us (7%)
  local copies, waits for them, and re-layouts  63.7 us (5%)
  starting transfers between devices  32.2 us (2%)
  other arithmetic  27.4 us (2%)
  between operations  15.9 us (1%)
    reduce_scatter x1, waiting for transfers between devices, per_device(): lax.psum_scatter(expert_down_term[:, None, :].astype(jnp.bfloat16), 'dp',...  148 us
    reduce_scatter x1, waiting for transfers between devices, per_device(): lax.psum_scatter(expert_up_term[:, None, :].astype(jnp.bfloat16), 'dp', s...  146 us
    all_gather x1, waiting for transfers between devices, fetch_weights(): lax.all_gather(expert_down, 'dp', axis=0, tiled=True)  117 us
    reduce_scatter x1, waiting for transfers between devices, per_device(): lax.psum_scatter(qkv_grad_rows.astype(jnp.bfloat16), 'dp', scatter_dimens...  66.2 us
    all_gather x1, blocking collectives, fetch_weights(): lax.all_gather(w_mix, ('dp', 'expert'), axis=0, tiled=True)  62.8 us
    reduce_scatter x1, waiting for transfers between devices, per_device(): lax.psum_scatter(down_grad_rows.astype(jnp.bfloat16), 'dp', scatter_dimen...  51.7 us
    all_gather x1, waiting for transfers between devices, fetch_weights(): lax.all_gather(w_up, 'dp', axis=0, tiled=True)  46 us
    all_gather x1, waiting for transfers between devices, fetch_weights(): lax.all_gather(w_down, 'dp', axis=0, tiled=True)  45.5 us
  transfers between devices with their start and end apart: 27, of which 16 were waited for; matrix products, arithmetic and copies ran while one was open for 12% of the time, Pallas kernels for 0%

commit v1 on v0

v1 whole, which is shorter than its diff:
```python
import jax
import jax.numpy as jnp
from jax import lax
from jax.sharding import PartitionSpec as P

HEAD = 64


EPS = 1e-05
NEG_FILL = -1e30
HIGHEST = lax.Precision.HIGHEST
ROWS_AXIS = (((0,), (0,)), ((), ()))
COLS_AXIS = (((1,), (1,)), ((), ()))


def layer_norm(values, norm_gain):
    row_mean = jnp.mean(values, axis=-1, keepdims=True)
    centered = values - row_mean
    inverse = lax.rsqrt(jnp.mean(centered * centered, axis=-1, keepdims=True) + EPS)
    normed = centered * inverse
    return (normed * norm_gain, normed, inverse)


def norm_back(grad_out, normed, inverse, norm_gain):
    scaled = grad_out * norm_gain
    mean_one = jnp.mean(scaled, axis=-1, keepdims=True)
    mean_two = jnp.mean(scaled * normed, axis=-1, keepdims=True)
    return (inverse * (scaled - mean_one - normed * mean_two), jnp.sum(grad_out * normed, axis=0))


def gelu_tanh(values):
    return jax.nn.gelu(values, approximate=True)


def gelu_back(pre_act, grad_act):
    return jax.vjp(gelu_tanh, pre_act)[1](grad_act)[0]


def softmax_rows(logits):
    shifted = logits - jnp.max(logits, axis=-1, keepdims=True)
    weights = jnp.exp(shifted)
    return weights / jnp.sum(weights, axis=-1, keepdims=True)


def contract_rows(left_side, right_side):
    return lax.dot_general(left_side, right_side, ROWS_AXIS, preferred_element_type=jnp.float32)


def contract_cols(left_side, right_side):
    return lax.dot_general(left_side, right_side, COLS_AXIS, preferred_element_type=jnp.float32)


def precise_rows(left_side, right_side):
    return lax.dot_general(
        left_side, right_side, ROWS_AXIS, precision=HIGHEST, preferred_element_type=jnp.float32
    )


def precise_cols(left_side, right_side):
    return lax.dot_general(
        left_side, right_side, COLS_AXIS, precision=HIGHEST, preferred_element_type=jnp.float32
    )


def per_device(
    tokens,
    cotangent,
    prefix,
    expert_choice,
    norm1_gain,
    w_qkv,
    w_out,
    norm2_gain,
    w_up,
    w_down,
    w_router,
    w_mix,
    expert_up,
    expert_down,
):
    local_rows, model_width = tokens.shape
    experts = lax.axis_size("expert")
    replicas = lax.axis_size("dp")
    capacity = 2 * local_rows // experts
    cut_width = model_width // experts
    head_count = cut_width // HEAD
    ff_cut = w_up.shape[1] // experts
    row_share = w_qkv.shape[0]
    ff_share = w_down.shape[0]
    stride = replicas // experts
    my_block = lax.axis_index("dp") * experts + lax.axis_index("expert")
    score_scale = HEAD ** (-0.5)

    ff_own = replicas * ff_share

    def spread(rows_low):
        return lax.all_gather(rows_low, "expert", axis=0, tiled=True)

    def fold(partial_sums):
        return lax.psum_scatter(
            partial_sums.astype(jnp.bfloat16), "expert", scatter_dimension=0, tiled=True
        ).astype(jnp.float32)

    def swap(blocks):
        return lax.all_to_all(blocks, "expert", split_axis=0, concat_axis=0, tiled=True)

    def gather_dp(rows):
        return lax.all_gather(rows, "dp", axis=0, tiled=True)

    def scatter_dp(rows):
        return lax.psum_scatter(
            rows.astype(jnp.bfloat16), "dp", scatter_dimension=0, tiled=True
        )

    small = lax.all_gather(
        jnp.concatenate([norm1_gain[:, None], norm2_gain[:, None], w_router, w_mix], axis=1),
        ("dp", "expert"),
        axis=0,
        tiled=True,
    )
    gain_one = small[:, 0].astype(jnp.float32)
    gain_two = small[:, 1].astype(jnp.float32)
    router_w = small[:, 2 : 2 + experts]
    mix_w = small[:, 2 + experts :]

    qkv_out = jnp.moveaxis(w_qkv.reshape(row_share, 3, experts, cut_width), 2, 0)
    qkv_w = gather_dp(swap(qkv_out).reshape(experts * row_share, 3 * cut_width))
    out_rows = gather_dp(w_out)
    out_in = swap(out_rows.reshape(experts, stride * row_share, model_width))
    out_w = jnp.transpose(
        out_in.reshape(experts, stride, row_share, model_width), (1, 0, 2, 3)
    ).reshape(cut_width, model_width)
    up_out = jnp.moveaxis(w_up.reshape(row_share, replicas, experts, ff_share), 2, 0)
    up_w = gather_dp(swap(up_out).reshape(experts * row_share, ff_own))
    down_w = gather_dp(w_down)
    expert_in_w = expert_up[:, 0, :]
    expert_out_w = expert_down[:, 0, :]

    inputs = tokens.astype(jnp.float32)
    scaled_one, normed_one, inverse_one = layer_norm(inputs, gain_one)
    normed_all = spread(scaled_one.astype(jnp.bfloat16))
    seq_len = normed_all.shape[0]
    qkv_cut = jnp.dot(normed_all, qkv_w, preferred_element_type=jnp.float32).astype(jnp.bfloat16)
    queries = qkv_cut[:, :cut_width].reshape(seq_len, head_count, HEAD)
    keys = qkv_cut[:, cut_width : 2 * cut_width].reshape(seq_len, head_count, HEAD)
    values = qkv_cut[:, 2 * cut_width :].reshape(seq_len, head_count, HEAD)
    position = jnp.arange(seq_len, dtype=jnp.int32)
    visible = (position[None, :] <= position[:, None]) | (position[None, :] < prefix[0])
    masked = jnp.where(
        visible[None],
        jnp.einsum("qhd,khd->hqk", queries, keys, preferred_element_type=jnp.float32)
        * score_scale,
        NEG_FILL,
    )
    row_max = jnp.max(masked, axis=-1, keepdims=True)
    expd = jnp.exp(masked - row_max)
    probs = expd / jnp.sum(expd, axis=-1, keepdims=True)
    probs_low = probs.astype(jnp.bfloat16)
    attended_cut = (
        jnp.einsum("hqk,khd->qhd", probs_low, values, preferred_element_type=jnp.float32)
        .reshape(seq_len, cut_width)
        .astype(jnp.bfloat16)
    )
    attn_out = fold(jnp.dot(attended_cut, out_w, preferred_element_type=jnp.float32))
    middle = inputs + attn_out
    scaled_two, normed_two, inverse_two = layer_norm(middle, gain_two)
    hidden_low = scaled_two.astype(jnp.bfloat16)
    router_probs = softmax_rows(jnp.dot(hidden_low, router_w, preferred_element_type=jnp.float32))
    chosen = expert_choice[:, 0]
    onehot_int = (jnp.arange(experts, dtype=jnp.int32)[None, :] == chosen[:, None]).astype(
        jnp.int32
    )
    onehot = onehot_int.astype(jnp.float32)
    gate_prob = jnp.sum(router_probs * onehot, axis=-1)
    mix_coef = softmax_rows(jnp.dot(hidden_low, mix_w, preferred_element_type=jnp.float32))
    coef_dense = mix_coef[:, 0:1]
    coef_expert = (mix_coef[:, 1] * gate_prob)[:, None]
    grad_out = cotangent.astype(jnp.float32)
    grad_dense = (grad_out * coef_dense).astype(jnp.bfloat16)
    grad_expert = (grad_out * coef_expert).astype(jnp.bfloat16)

    row_id = jnp.arange(local_rows, dtype=jnp.int32)
    before = (row_id[:, None] > row_id[None, :]).astype(jnp.bfloat16)
    earlier = jnp.dot(before, onehot.astype(jnp.bfloat16), preferred_element_type=jnp.float32)
    slot_rank = jnp.sum(earlier * onehot, axis=-1).astype(jnp.int32)
    slot_index = chosen * capacity + slot_rank
    slot_rows = experts * capacity
    picks = (slot_index[:, None] == jnp.arange(slot_rows, dtype=jnp.int32)[None, :]).astype(
        jnp.bfloat16
    )
    send_rows = contract_rows(picks, jnp.concatenate([hidden_low, grad_expert], axis=1)).astype(
        jnp.bfloat16
    )
    received = swap(send_rows.reshape(experts, capacity, 2 * model_width))
    routed = gather_dp(received.reshape(slot_rows, 2 * model_width))
    routed_in = routed[:, :model_width]
    routed_grad = routed[:, model_width:]
    dense_rows = spread(jnp.concatenate([hidden_low, grad_dense], axis=1))
    hidden_all = dense_rows[:, :model_width]
    grad_dense_all = dense_rows[:, model_width:]

    dense_pre = jnp.dot(hidden_all, up_w, preferred_element_type=jnp.float32)
    dense_act = gelu_tanh(dense_pre).astype(jnp.bfloat16)
    grad_act_d = contract_cols(grad_dense_all, down_w)
    grad_pre_d = gelu_back(dense_pre, grad_act_d).astype(jnp.bfloat16)
    dense_sums = jnp.concatenate(
        [
            jnp.dot(dense_act, down_w, preferred_element_type=jnp.float32).astype(jnp.bfloat16),
            contract_cols(grad_pre_d, up_w).astype(jnp.bfloat16),
        ],
        axis=1,
    )
    dense_back = fold(dense_sums)
    dense_out = dense_back[:, :model_width]
    grad_w_down_cut = contract_rows(dense_act, grad_dense_all)
    grad_w_up_cut = contract_rows(hidden_all, grad_pre_d)

    pre_act = contract_cols(routed_in, expert_in_w)
    act_low = gelu_tanh(pre_act).astype(jnp.bfloat16)
    grad_act_e = contract_cols(routed_grad, expert_out_w)
    grad_pre_e = gelu_back(pre_act, grad_act_e).astype(jnp.bfloat16)
    expert_sums = jnp.concatenate(
        [
            jnp.dot(act_low, expert_out_w, preferred_element_type=jnp.float32).astype(
                jnp.bfloat16
            ),
            jnp.dot(grad_pre_e, expert_in_w, preferred_element_type=jnp.float32).astype(
                jnp.bfloat16
            ),
        ],
        axis=1,
    )
    grad_expert_up = contract_rows(grad_pre_e, routed_in)
    grad_expert_down = contract_rows(act_low, routed_grad)
    expert_back = swap(scatter_dp(expert_sums).reshape(experts, capacity, 2 * model_width))
    expert_rows_all = jnp.dot(
        picks, expert_back.reshape(slot_rows, 2 * model_width), preferred_element_type=jnp.float32
    )
    expert_rows = expert_rows_all[:, :model_width]

    ffn_out = coef_dense * dense_out + coef_expert * expert_rows
    result = middle + ffn_out
    square_stats = jnp.stack(
        [
            jnp.sum(middle * middle),
            jnp.sum(attn_out * attn_out),
            jnp.sum(ffn_out * ffn_out),
            jnp.sum(result * result),
        ]
    )
    dense_dot = jnp.sum(grad_out * dense_out, axis=-1)
    expert_dot = jnp.sum(grad_out * expert_rows, axis=-1)
    coef_grad = jnp.stack([dense_dot, expert_dot * gate_prob], axis=-1)
    grad_mix = mix_coef * (coef_grad - jnp.sum(mix_coef * coef_grad, axis=-1, keepdims=True))
    gate_grad = expert_dot * mix_coef[:, 1]
    grad_router = (gate_grad * gate_prob)[:, None] * (onehot - router_probs)

    hidden_wide = hidden_low.astype(jnp.float32)
    grad_hidden = dense_back[:, model_width:] + expert_rows_all[:, model_width:]
    grad_hidden = (
        grad_hidden
        + precise_cols(grad_router, router_w.astype(jnp.float32))
        + precise_cols(grad_mix, mix_w.astype(jnp.float32))
    )
    grad_w_router = precise_rows(grad_router, hidden_wide)
    grad_w_mix = precise_rows(grad_mix, hidden_wide)
    grad_mid_norm, grad_gain_two = norm_back(grad_hidden, normed_two, inverse_two, gain_two)
    grad_middle = grad_out + grad_mid_norm
    grad_attn_all = spread(grad_middle.astype(jnp.bfloat16))
    grad_w_out_cut = contract_rows(attended_cut, grad_attn_all)
    grad_att_cut = (
        contract_cols(grad_attn_all, out_w)
        .astype(jnp.bfloat16)
        .reshape(seq_len, head_count, HEAD)
    )

    grad_probs = jnp.einsum(
        "qhd,khd->hqk", grad_att_cut, values, preferred_element_type=jnp.float32
    )
    row_delta = jnp.sum(probs * grad_probs, axis=-1, keepdims=True)
    grad_scores = (probs * (grad_probs - row_delta)).astype(jnp.bfloat16)
    grad_query = (
        jnp.einsum("hqk,khd->qhd", grad_scores, keys, preferred_element_type=jnp.float32)
        * score_scale
    )
    grad_key = (
        jnp.einsum("hqk,qhd->khd", grad_scores, queries, preferred_element_type=jnp.float32)
        * score_scale
    )
    grad_value = jnp.einsum(
        "hqk,qhd->khd", probs_low, grad_att_cut, preferred_element_type=jnp.float32
    )
    grad_qkv_cut = jnp.concatenate(
        [
            grad_query.reshape(seq_len, cut_width),
            grad_key.reshape(seq_len, cut_width),
            grad_value.reshape(seq_len, cut_width),
        ],
        axis=1,
    ).astype(jnp.bfloat16)
    grad_w_qkv_cut = contract_rows(normed_all, grad_qkv_cut)
    grad_normed = fold(contract_cols(grad_qkv_cut, qkv_w))
    grad_in_norm, grad_gain_one = norm_back(grad_normed, normed_one, inverse_one, gain_one)
    grad_tokens = grad_middle + grad_in_norm

    up_sum = swap(
        scatter_dp(grad_w_up_cut).reshape(experts, row_share, replicas, ff_share)
    )
    grad_w_up = (
        jnp.transpose(up_sum, (1, 2, 0, 3)).reshape(row_share, experts * ff_own)
    ).astype(jnp.float32)
    grad_w_down = scatter_dp(grad_w_down_cut).astype(jnp.float32)
    out_send = jnp.transpose(
        grad_w_out_cut.astype(jnp.bfloat16).reshape(stride, experts, row_share, model_width),
        (1, 0, 2, 3),
    )
    grad_w_out = scatter_dp(swap(out_send).reshape(replicas * row_share, model_width)).astype(
        jnp.float32
    )
    qkv_sum = swap(scatter_dp(grad_w_qkv_cut).reshape(experts, row_share, 3, cut_width))
    grad_w_qkv = (
        jnp.transpose(qkv_sum, (1, 2, 0, 3)).reshape(row_share, 3 * model_width)
    ).astype(jnp.float32)

    totals = lax.psum(
        (
            jnp.concatenate(
                [grad_gain_one[None], grad_gain_two[None], grad_w_router, grad_w_mix], axis=0
            ),
            square_stats,
        ),
        ("dp", "expert"),
    )
    own = lax.dynamic_slice_in_dim(totals[0], my_block * row_share, row_share, 1)
    entry_count = local_rows * model_width * replicas * experts
    rms_values = jnp.sqrt(totals[1] / entry_count + 1e-06)
    return (
        result,
        grad_tokens,
        own[0],
        grad_w_qkv,
        grad_w_out,
        own[1],
        grad_w_up,
        grad_w_down,
        jnp.transpose(own[2 : 2 + experts]),
        jnp.transpose(own[2 + experts :]),
        grad_expert_up[:, None, :],
        grad_expert_down[:, None, :],
        rms_values[0],
        rms_values[1],
        rms_values[2],
        rms_values[3],
    )


def solution(mesh):
    return jax.shard_map(
        per_device,
        mesh=mesh,
        in_specs=(
            P(("dp", "expert"), None),
            P(("dp", "expert"), None),
            P("dp"),
            P(("dp", "expert"), None),
            P(("dp", "expert")),
            P(("dp", "expert"), None),
            P(("dp", "expert"), None),
            P(("dp", "expert")),
            P(("dp", "expert"), None),
            P(("dp", "expert"), None),
            P(("dp", "expert"), None),
            P(("dp", "expert"), None),
            P("dp", "expert", None),
            P("dp", "expert", None),
        ),
        out_specs=(
            P(("dp", "expert"), None),
            P(("dp", "expert"), None),
            P(("dp", "expert")),
            P(("dp", "expert"), None),
            P(("dp", "expert"), None),
            P(("dp", "expert")),
            P(("dp", "expert"), None),
            P(("dp", "expert"), None),
            P(("dp", "expert"), None),
            P(("dp", "expert"), None),
            P("dp", "expert", None),
            P("dp", "expert", None),
            P(),
            P(),
            P(),
            P(),
        ),
        check_vma=False,
    )
```

time: 1290 us -> 958 us (0.74)
  blocking collectives: 316 us -> 153 us
  waiting for transfers between devices: 740 us -> 627 us
  local copies, waits for them, and re-layouts: 63.7 us -> 25.2 us
  starting transfers between devices: 32.2 us -> 18.8 us
    all_to_all x4 -> x3, blocking collectives: 96.2 us -> 36.1 us  [swap(): lax.all_to_all(blocks, 'expert', split_axis=0, concat_axis=0, tiled=True)]
    all_gather x3 -> x2, blocking collectives: 137 us -> 77.2 us  [the longest x1 43.4 us: per_device(): lax.all_gather(jnp.concatenate([norm1_gain[:, None], norm2_gain[:, None],...]
    reduce_scatter x10 -> x8, waiting for transfers between devices: 439 us -> 395 us  [the longest x5 320 us: scatter_dp(): lax.psum_scatter(rows.astype(jnp.bfloat16), 'dp', scatter_dimension=0, ti...]
    all_gather x5 -> x4, waiting for transfers between devices: 228 us -> 185 us  [gather_dp(): return lax.all_gather(rows, 'dp', axis=0, tiled=True)]
    unnamed x1 -> x0, blocking collectives: 41.7 us -> none
    all_to_all x8 -> x5, waiting for transfers between devices: 38.4 us -> 14.6 us  [swap(): lax.all_to_all(blocks, 'expert', split_axis=0, concat_axis=0, tiled=True)]
    dot_general x12 -> x11, matrix products: 45.8 us -> 23 us  [the longest x1 4.43 us: per_device(): jnp.dot(grad_pre_e, expert_in_w, preferred_element_type=jnp.float32)]
    all_to_all x8 -> x5, starting transfers between devices: 30.9 us -> 17.4 us  [swap(): lax.all_to_all(blocks, 'expert', split_axis=0, concat_axis=0, tiled=True)]
  transfers between devices with their start and end apart: 27 -> 20, of which waited for: 16 -> 17; matrix products, arithmetic and copies ran while one was open for 12% -> 11% of each run, Pallas kernels for 0% -> 0%
where the time goes in v1:
time: 958 us; the launch traced here: 952 us
  waiting for transfers between devices  627 us (65%)
  blocking collectives  153 us (16%)
  matrix products  78 us (8%)
  other arithmetic  34 us (4%)
  local copies, waits for them, and re-layouts  25.2 us (3%)
  starting transfers between devices  18.8 us (2%)
  between operations  15.6 us (2%)
    reduce_scatter x5, waiting for transfers between devices, scatter_dp(): lax.psum_scatter(rows.astype(jnp.bfloat16), 'dp', scatter_dimension=0, ti...  320 us
    all_gather x4, waiting for transfers between devices, gather_dp(): return lax.all_gather(rows, 'dp', axis=0, tiled=True)  185 us
    reduce_scatter x3, waiting for transfers between devices, fold(): lax.psum_scatter(partial_sums.astype(jnp.bfloat16), 'expert', scatter_dim...  75.4 us
    all_gather x1, blocking collectives, per_device(): lax.all_gather(jnp.concatenate([norm1_gain[:, None], norm2_gain[:, None],...  43.4 us
    psum x1, blocking collectives, per_device(): lax.psum((jnp.concatenate([grad_gain_one[None], grad_gain_two[None], grad...  39.9 us
    all_to_all x3, blocking collectives, swap(): lax.all_to_all(blocks, 'expert', split_axis=0, concat_axis=0, tiled=True)  36.1 us
    all_gather x1, blocking collectives, gather_dp(): return lax.all_gather(rows, 'dp', axis=0, tiled=True)  33.8 us
    all_gather x3, waiting for transfers between devices, spread(): return lax.all_gather(rows_low, 'expert', axis=0, tiled=True)  31.6 us
  transfers between devices with their start and end apart: 20, of which 17 were waited for; matrix products, arithmetic and copies ran while one was open for 11% of the time, Pallas kernels for 0%

profile of v1, /device:TPU:0, one launch (start us, length us, event | category | flops | bytes accessed | tf_op | source)
XLA Modules:
  0.0 951.5 jit_solution(9734725191694061075)
XLA Ops:
  10.3 43.4 %all-gather = bf16[32,32,8]{1,2,0:T(8,128)(2,1)S(1)} all-gather(bf16[1,32,8]{1,2,0:T(8,128)(2,1)S(1)} %maximum_bitcast_fusion), channel_id=1, replica_groups=mesh['dp'=8,'expert'=4] {'dp','expert'}, dimensions={0}, use_global_device_ids=true | all-gather | bytes 16896 | tf_op jit(solution)/shard_map/all_gather | solution.py:115
  56.9 10.1 %all_to_all.40 = bf16[4,32,3,256]{3,1,2,0:T(8,128)(2,1)S(1)} all-to-all(bf16[4,32,3,256]{3,1,2,0:T(8,128)(2,1)S(1)} %copy.96), channel_id=1, replica_groups=mesh['dp'=8,'expert'=4] {'expert'}, dimensions={0} | all-to-all | bytes 393216 | tf_op jit(solution)/shard_map/all_to_all | solution.py:105
  67.9 33.8 %all_gather.30 = bf16[256,1024]{1,0:T(8,128)(2,1)} all-gather(bf16[32,1024]{1,0:T(8,128)(2,1)S(1)} %copy-done.26), channel_id=1, replica_groups=mesh['dp'=8,'expert'=4] {'dp'}, dimensions={0}, use_global_device_ids=true | all-gather | bytes 589824 | tf_op jit(solution)/shard_map/all_gather | solution.py:108
  106.0 7.9 all-to-all-done.1
  128.3 23.1 %reduce-scatter.9.cloned.1.call-done = bf16[128,1024]{1,0:T(8,128)(2,1)} async-done(((bf16[512,1024]{1,0:T(8,128)(2,1)}), bf16[128,1024]{1,0:T(8,128)(2,1)}) %reduce-scatter.9.cloned.1.call-update) | async-done | bytes 262160 | tf_op jit(solution)/shard_map/reduce_scatter | solution.py:100
  156.1 17.6 %all_to_all.41 = bf16[4,64,2048]{2,1,0:T(8,128)(2,1)} all-to-all(bf16[4,64,2048]{2,1,0:T(8,128)(2,1)S(1)} %bitcast.155), channel_id=1, replica_groups=mesh['dp'=8,'expert'=4] {'expert'}, dimensions={0} | all-to-all | bytes 2097152 | tf_op jit(solution)/shard_map/all_to_all | solution.py:105
  174.0 8.4 all_to_all.42
  185.1 113.2 %all-gather.19.cloned.1.call-done = bf16[2048,2048]{1,0:T(8,128)(2,1)} async-done(((bf16[256,2048]{1,0:T(8,128)(2,1)}), bf16[2048,2048]{1,0:T(8,128)(2,1)}) %all-gather.19.cloned.1.call-update) | async-done | bytes 8388624 | tf_op jit(solution)/shard_map/all_gather | solution.py:108
  298.3 4.8 fusion.14
  303.1 5.0 fusion.7
  316.8 8.4 pad_maximum_fusion
  325.7 22.5 %all-gather.15.cloned.1.call-done = bf16[1024,1024]{1,0:T(8,128)(2,1)} async-done(((bf16[128,1024]{1,0:T(8,128)(2,1)}), bf16[1024,1024]{1,0:T(8,128)(2,1)}) %all-gather.15.cloned.1.call-update) | async-done | bytes 2097168 | tf_op jit(solution)/shard_map/all_gather | solution.py:108
  348.2 23.1 %all-gather.13.cloned.1.call-done = bf16[512,2048]{1,0:T(8,128)(2,1)} async-done(((bf16[128,2048]{1,0:T(8,128)(2,1)}), bf16[512,2048]{1,0:T(8,128)(2,1)}) %all-gather.13.cloned.1.call-update) | async-done | bytes 2097168 | tf_op jit(solution)/shard_map/all_gather | solution.py:97
  375.9 46.6 %all-gather.17.cloned.1.call-done = bf16[1024,1024]{1,0:T(8,128)(2,1)} async-done(((bf16[128,1024]{1,0:T(8,128)(2,1)}), bf16[1024,1024]{1,0:T(8,128)(2,1)}) %all-gather.17.cloned.1.call-update) | async-done | bytes 2097168 | tf_op jit(solution)/shard_map/all_gather | solution.py:108
  432.9 139.7 %reduce-scatter.13.cloned.1.call-done = bf16[256,2048]{0,1:T(8,128)(2,1)} async-done(((bf16[2048,2048]{0,1:T(8,128)(2,1)}), bf16[256,2048]{0,1:T(8,128)(2,1)}) %reduce-scatter.13.cloned.1.call-update) | async-done | bytes 1048592 | tf_op jit(solution)/shard_map/reduce_scatter | solution.py:111
  578.4 27.6 %reduce-scatter.11.cloned.1.call-done = bf16[128,2048]{1,0:T(8,128)(2,1)} async-done(((bf16[512,2048]{1,0:T(8,128)(2,1)}), bf16[128,2048]{1,0:T(8,128)(2,1)}) %reduce-scatter.11.cloned.1.call-update) | async-done | bytes 524304 | tf_op jit(solution)/shard_map/reduce_scatter | solution.py:100
  620.7 8.4 all-gather.21.cloned.1.call-done
  650.6 51.2 %reduce-scatter.21.cloned.1.call-done = bf16[128,1024]{1,0:T(8,128)(2,1)} async-done(((bf16[1024,1024]{1,0:T(8,128)(2,1)}), bf16[128,1024]{1,0:T(8,128)(2,1)}) %reduce-scatter.21.cloned.1.call-update) | async-done | bytes 262160 | tf_op jit(solution)/shard_map/reduce_scatter | solution.py:111
  707.2 65.6 %reduce-scatter.23.cloned.1.call-done = bf16[128,1024]{1,0:T(8,128)(2,1)} async-done(((bf16[1024,1024]{1,0:T(8,128)(2,1)}), bf16[128,1024]{1,0:T(8,128)(2,1)}) %reduce-scatter.23.cloned.1.call-update) | async-done | bytes 262160 | tf_op jit(solution)/shard_map/reduce_scatter | solution.py:111
  778.3 5.9 fusion.32
  798.9 39.1 %reduce-scatter.19.cloned.1.call-done = bf16[32,1024]{1,0:T(8,128)(2,1)} async-done(((bf16[256,1024]{1,0:T(8,128)(2,1)}), bf16[32,1024]{1,0:T(8,128)(2,1)}) %reduce-scatter.19.cloned.1.call-update) | async-done | bytes 65552 | tf_op jit(solution)/shard_map/reduce_scatter | solution.py:111
  839.5 24.7 %reduce-scatter.15.cloned.1.call-done = bf16[128,1024]{1,0:T(8,128)(2,1)} async-done(((bf16[512,1024]{1,0:T(8,128)(2,1)}), bf16[128,1024]{1,0:T(8,128)(2,1)}) %reduce-scatter.15.cloned.1.call-update) | async-done | bytes 262160 | tf_op jit(solution)/shard_map/reduce_scatter | solution.py:100
  865.4 39.9 %all-reduce = (f32[8,1024]{1,0:T(8,128)S(1)}, f32[4]{0:T(128)S(1)}) all-reduce(f32[8,1024]{1,0:T(8,128)S(1)} %pad_maximum_fusion.8, f32[4]{0:T(128)S(1)} %pad_maximum_fusion.10), channel_id=1, replica_groups=mesh['dp'=8,'expert'=4] {'dp','expert'}, use_global_device_ids=true, to_apply=%region_26.27 | all-reduce | flops 8196 | bytes 65568 | tf_op jit(solution)/shard_map/psum | solution.py:325
  909.2 24.0 %reduce-scatter.17.cloned.1.call-done = bf16[128,768]{1,0:T(8,128)(2,1)} async-done(((bf16[1024,768]{1,0:T(8,128)(2,1)}), bf16[128,768]{1,0:T(8,128)(2,1)}) %reduce-scatter.17.cloned.1.call-update) | async-done | bytes 196624 | tf_op jit(solution)/shard_map/reduce_scatter | solution.py:111
  (226 shorter events, 141.9 us)
Async XLA Ops:
  7.2 291.2 %copy-start = (bf16[512,1,1024]{2,0,1:T(8,128)(2,1)S(1)}, bf16[512,1,1024]{2,0,1:T(8,128)(2,1)}, u32[]{:S(2)}) copy-start(bf16[512,1,1024]{2,0,1:T(8,128)(2,1)} %param.26) | copy-start | bytes 3145732
  7.2 106.8 %all-gather.9.cloned.1.call-start = ((), (), s32[]{:S(2)}) async-start(), calls=%async_computation.16 | async-start | bytes 1310720 | tf_op jit(solution)/shard_map/all_gather | solution.py:97
  55.8 60.6 %all-gather.11.cloned.1.call-start = ((), (), s32[]{:S(2)}) async-start(), calls=%async_computation.17 | async-start | bytes 1769472 | tf_op jit(solution)/shard_map/all_gather | solution.py:108
  101.7 12.3 %all-to-all-start.1 = ((bf16[4,64,1024]{2,1,0:T(8,128)(2,1)}), bf16[4,64,1024]{2,1,0:T(8,128)(2,1)S(1)}, u32[]{:S(2)}, u32[]{:S(2)}) async-start(bf16[4,64,1024]{2,1,0:T(8,128)(2,1)} %bitcast.11), calls=%async_computation.1 | async-start | bytes 1048576 | tf_op jit(solution)/shard_map/all_to_all | solution.py:105
  105.2 46.3 %reduce-scatter.9.cloned.1.call-start = ((), (), s32[]{:S(2)}) async-start(), calls=%async_computation.18 | async-start | bytes 1310720 | tf_op jit(solution)/shard_map/reduce_scatter | solution.py:100
  128.1 170.2 %all-gather.19.cloned.1.call-start = ((), (), s32[]{:S(2)}) async-start(), calls=%async_computation.23 | async-start | bytes 9437184 | tf_op jit(solution)/shard_map/all_gather | solution.py:108
  173.7 174.5 %all-gather.15.cloned.1.call-start = ((), (), s32[]{:S(2)}) async-start(), calls=%async_computation.20 | async-start | bytes 2359296 | tf_op jit(solution)/shard_map/all_gather | solution.py:108
  183.2 188.1 %all-gather.13.cloned.1.call-start = ((), (), s32[]{:S(2)}) async-start(), calls=%async_computation.19 | async-start | bytes 2621440 | tf_op jit(solution)/shard_map/all_gather | solution.py:97
  184.1 238.5 %all-gather.17.cloned.1.call-start = ((), (), s32[]{:S(2)}) async-start(), calls=%async_computation.21 | async-start | bytes 2359296 | tf_op jit(solution)/shard_map/all_gather | solution.py:108
  184.8 118.3 %copy-start.34 = (bf16[512,1,1024]{2,0,1:T(8,128)(2,1)S(1)}, bf16[512,1,1024]{2,0,1:T(8,128)(2,1)}, u32[]{:S(2)}) copy-start(bf16[512,1,1024]{2,0,1:T(8,128)(2,1)} %param.27) | copy-start | bytes 3145732
  184.8 387.7 %reduce-scatter.13.cloned.1.call-start = ((), (), s32[]{:S(2)}) async-start(), calls=%async_computation.24 | async-start | bytes 9437184 | tf_op jit(solution)/shard_map/reduce_scatter | solution.py:111
  325.2 280.8 %reduce-scatter.11.cloned.1.call-start = ((), (), s32[]{:S(2)}) async-start(), calls=%async_computation.22 | async-start | bytes 2621440 | tf_op jit(solution)/shard_map/reduce_scatter | solution.py:100
  574.8 32.3 %all-to-all-start.4 = ((bf16[4,64,2048]{2,1,0:T(8,128)(2,1)}), bf16[4,64,2048]{2,1,0:T(8,128)(2,1)S(1)}, u32[]{:S(2)}, u32[]{:S(2)}) async-start(bf16[4,64,2048]{2,1,0:T(8,128)(2,1)} %bitcast.27), calls=%async_computation.7 | async-start | bytes 2097152 | tf_op jit(solution)/shard_map/all_to_all | solution.py:105
  578.4 50.7 %all-gather.21.cloned.1.call-start = ((), (), s32[]{:S(2)}) async-start(), calls=%async_computation.25 | async-start | bytes 1310720 | tf_op jit(solution)/shard_map/all_gather | solution.py:97
  612.2 89.5 %reduce-scatter.21.cloned.1.call-start = ((), (), s32[]{:S(2)}) async-start(), calls=%async_computation.29 | async-start | bytes 2359296 | tf_op jit(solution)/shard_map/reduce_scatter | solution.py:111
  616.1 156.7 %reduce-scatter.23.cloned.1.call-start = ((), (), s32[]{:S(2)}) async-start(), calls=%async_computation.30 | async-start | bytes 2359296 | tf_op jit(solution)/shard_map/reduce_scatter | solution.py:111
  631.7 12.3 %all-to-all-start.6 = ((bf16[4,2,32,1024]{3,2,1,0:T(8,128)(2,1)}), bf16[4,2,32,1024]{3,2,1,0:T(8,128)(2,1)S(1)}, u32[]{:S(2)}, u32[]{:S(2)}) async-start(bf16[4,2,32,1024]{3,2,1,0:T(8,128)(2,1)} %bitcast.149), calls=%async_computation.11 | async-start | bytes 1048576 | tf_op jit(solution)/shard_map/all_to_all | solution.py:105
  635.2 202.8 %reduce-scatter.19.cloned.1.call-start = ((), (), s32[]{:S(2)}) async-start(), calls=%async_computation.28 | async-start | bytes 589824 | tf_op jit(solution)/shard_map/reduce_scatter | solution.py:111
  644.7 219.4 %reduce-scatter.15.cloned.1.call-start = ((), (), s32[]{:S(2)}) async-start(), calls=%async_computation.26 | async-start | bytes 1310720 | tf_op jit(solution)/shard_map/reduce_scatter | solution.py:100
  703.5 72.5 %copy-start.35 = (bf16[512,1024]{1,0:T(8,128)(2,1)S(1)}, bf16[512,1024]{1,0:T(8,128)(2,1)}, u32[]{:S(2)}) copy-start(bf16[512,1024]{1,0:T(8,128)(2,1)} %all-gather.9.cloned.1.call-done) | copy-start | bytes 3145732
  703.5 71.1 %all-to-all-start.7 = ((bf16[4,32,8,128]{3,2,1,0:T(8,128)(2,1)}), bf16[4,32,8,128]{3,2,1,0:T(8,128)(2,1)S(1)}, u32[]{:S(2)}, u32[]{:S(2)}) async-start(bf16[4,32,8,128]{3,2,1,0:T(8,128)(2,1)} %bitcast.74), calls=%async_computation.14 | async-start | bytes 524288 | tf_op jit(solution)/shard_map/all_to_all | solution.py:105
  707.0 226.2 %reduce-scatter.17.cloned.1.call-start = ((), (), s32[]{:S(2)}) async-start(), calls=%async_computation.27 | async-start | bytes 1769472 | tf_op jit(solution)/shard_map/reduce_scatter | solution.py:111
  792.3 114.9 %copy-start.11 = (f32[128,1024]{1,0:T(8,128)S(1)}, f32[128,1024]{1,0:T(8,128)}, u32[]{:S(2)}) copy-start(f32[128,1024]{1,0:T(8,128)} %get-tuple-element.112) | copy-start | bytes 1572868
  934.9 8.6 all-to-all-start.5
  (38 other events, 504.4 us)
Sparse Core Ops, SparseCore 0:
  55.9 14.9 all-gather.8
  73.6 42.6 all-gather.10
  128.2 23.2 reduce-scatter.8
  173.8 124.4 all-gather.18
  300.9 47.2 all-gather.14
  350.2 21.0 all-gather.12
  373.4 49.0 all-gather.16
  426.2 146.3 reduce-scatter.12
  575.7 30.2 reduce-scatter.10
  612.3 16.6 all-gather.20
  633.2 68.5 reduce-scatter.20
  705.1 67.6 reduce-scatter.22
  776.1 61.7 reduce-scatter.18
  840.3 23.7 reduce-scatter.14
  867.4 65.7 reduce-scatter.16

commit v2 on v1

--- a/solution.py
+++ b/solution.py
@@ -1,6 +1,10 @@
+import functools
+
 import jax
 import jax.numpy as jnp
 from jax import lax
+from jax.experimental import pallas as pl
+from jax.experimental.pallas import tpu as pltpu
 from jax.sharding import PartitionSpec as P
 
 HEAD = 64
@@ -60,6 +64,394 @@
     return lax.dot_general(
         left_side, right_side, COLS_AXIS, precision=HIGHEST, preferred_element_type=jnp.float32
     )
+
+
+MESH = pl.DeviceIdType.MESH
+VMEM_SPEC = pl.BlockSpec(memory_space=pltpu.VMEM)
+ANY_SPEC = pl.BlockSpec(memory_space=pl.ANY)
+GRANT = 60 * 1024 * 1024
+
+
+def comm_params(call_id):
+    return pltpu.CompilerParams(
+        collective_id=call_id, has_side_effects=True, vmem_limit_bytes=GRANT
+    )
+
+
+def remote(src, dst, send_sem, recv_sem, device):
+    return pltpu.make_async_remote_copy(
+        src_ref=src,
+        dst_ref=dst,
+        send_sem=send_sem,
+        recv_sem=recv_sem,
+        device_id=device,
+        device_id_type=MESH,
+    )
+
+
+def exchange_kernel(axis, outer, inner, gathers, swaps, *refs):
+    count = outer * inner
+    total = gathers + swaps
+    ins, outs = refs[:total], refs[total : 2 * total]
+    send, recv, local, swap_send = refs[2 * total :]
+    me = lax.axis_index(axis)
+    row, col = me // inner, me % inner
+    barrier = pltpu.get_barrier_semaphore()
+    if swaps:
+        for step in range(1, count):
+            pl.semaphore_signal(
+                barrier, inc=1, device_id={axis: (me + step) % count}, device_id_type=MESH
+            )
+        pl.semaphore_wait(barrier, count - 1)
+    else:
+        for has, peer in ways(row, col, outer, inner, me):
+
+            @pl.when(has)
+            def _(peer=peer):
+                pl.semaphore_signal(barrier, inc=1, device_id={axis: peer}, device_id_type=MESH)
+
+        pl.semaphore_wait(barrier, neighbours(row, col, outer, inner))
+
+    def hop(item, index, src, way, peer):
+        return remote(
+            src,
+            outs[item].at[index],
+            send.at[item, way, index],
+            recv.at[item, index],
+            {axis: peer},
+        )
+
+    links = ways(row, col, outer, inner, me)
+    started = []
+
+    def start(item, index, src, way, extra):
+        has, peer = links[way]
+        cond = has if extra is None else jnp.logical_and(has, extra)
+
+        @pl.when(cond)
+        def _():
+            hop(item, index, src, way, peer).start()
+
+        started.append((item, index, src, way, cond))
+
+    def arrived(item, index):
+        hop(item, index, outs[item].at[index], 0, me).wait_recv()
+
+    own = []
+    for item in range(gathers):
+        copy = pltpu.make_async_copy(ins[item], outs[item].at[me], local.at[item])
+        for way in range(4):
+            start(item, me, ins[item], way, None)
+        copy.start()
+        own.append(copy)
+    for slot in range(swaps):
+        item = gathers + slot
+        for step in range(1, count):
+            peer = (me + step) % count
+            remote(
+                ins[item].at[peer],
+                outs[item].at[me],
+                swap_send.at[slot, step],
+                recv.at[item, me],
+                {axis: peer},
+            ).start()
+        copy = pltpu.make_async_copy(ins[item].at[me], outs[item].at[me], local.at[item])
+        copy.start()
+        own.append(copy)
+    for item in range(gathers):
+        for far in range(1, outer):
+            for sign, onward in ((-1, 0), (1, 1)):
+                source = row + sign * far
+                valid = jnp.logical_and(source >= 0, source < outer)
+                index = jnp.clip(source, 0, outer - 1) * inner + col
+
+                @pl.when(valid)
+                def _(item=item, index=index):
+                    arrived(item, index)
+
+                for way in (onward, 2, 3):
+                    start(item, index, outs[item].at[index], way, valid)
+    for item in range(gathers):
+        for source in range(outer):
+            arrived(item, source * inner + 1 - col)
+    for slot in range(swaps):
+        item = gathers + slot
+        for step in range(1, count):
+            arrived(item, (me + step) % count)
+    for copy in own:
+        copy.wait()
+    for item, index, src, way, cond in started:
+
+        @pl.when(cond)
+        def _(item=item, index=index, src=src, way=way):
+            hop(item, index, src, way, me).wait_send()
+
+    for slot in range(swaps):
+        item = gathers + slot
+        for step in range(1, count):
+            remote(
+                ins[item].at[(me + step) % count],
+                outs[item].at[me],
+                swap_send.at[slot, step],
+                recv.at[item, me],
+                {axis: me},
+            ).wait_send()
+
+
+def ways(row, col, outer, inner, me):
+    count = outer * inner
+    return (
+        (row < outer - 1, jnp.minimum(me + inner, count - 1)),
+        (row > 0, jnp.maximum(me - inner, 0)),
+        (col < inner - 1, jnp.minimum(me + 1, count - 1)),
+        (col > 0, jnp.maximum(me - 1, 0)),
+    )
+
+
+def neighbours(row, col, outer, inner):
+    return (
+        4
+        - (row == 0).astype(jnp.int32)
+        - (row == outer - 1).astype(jnp.int32)
+        - (col == 0).astype(jnp.int32)
+        - (col == inner - 1).astype(jnp.int32)
+    )
+
+
+def exchange(axis, outer, call_id, gathers=(), swaps=()):
+    count = lax.axis_size(axis)
+    inner = count // outer
+    items = tuple(gathers) + tuple(swaps)
+    shapes = [(count,) + item.shape for item in gathers] + [item.shape for item in swaps]
+    outs = pl.pallas_call(
+        functools.partial(exchange_kernel, axis, outer, inner, len(gathers), len(swaps)),
+        out_shape=[
+            jax.ShapeDtypeStruct(shape, item.dtype) for shape, item in zip(shapes, items)
+        ],
+        in_specs=[VMEM_SPEC] * len(items),
+        out_specs=[ANY_SPEC] * len(items),
+        scratch_shapes=[
+            pltpu.SemaphoreType.DMA((max(1, len(gathers)), 4, count)),
+            pltpu.SemaphoreType.DMA((len(items), count)),
+            pltpu.SemaphoreType.DMA((len(items),)),
+            pltpu.SemaphoreType.DMA((max(1, len(swaps)), count)),
+        ],
+        compiler_params=comm_params(call_id),
+        name=f"exchange_{call_id}",
+    )(*items)
+    return outs
+
+
+def add_rows(target, first, second, start, rows):
+    step = 16
+
+    def body(index, carry):
+        where = pl.ds(pl.multiple_of(start + index * step, step), step)
+        target[where, :] = (
+            first[where, :].astype(jnp.float32) + second[where, :].astype(jnp.float32)
+        ).astype(target.dtype)
+        return carry
+
+    lax.fori_loop(0, rows // step, body, 0)
+
+
+def reduce_kernel(axis, outer, items, parts, *refs):
+    inner = 2
+    count = outer * inner
+    ins, outs = refs[:items], refs[items : 2 * items]
+    scratch = refs[2 * items :]
+    near, held, above, below = (scratch[k * items : (k + 1) * items] for k in range(4))
+    near_send, near_recv, far_send, up_recv, down_recv = scratch[4 * items :]
+    me = lax.axis_index(axis)
+    row, col = me // inner, me % inner
+    partner = me + 1 - 2 * col
+    links = ways(row, col, outer, inner, me)
+    barrier = pltpu.get_barrier_semaphore()
+    for has, peer in links:
+
+        @pl.when(has)
+        def _(peer=peer):
+            pl.semaphore_signal(barrier, inc=1, device_id={axis: peer}, device_id_type=MESH)
+
+    pl.semaphore_wait(barrier, neighbours(row, col, outer, inner))
+
+    high = row >= (outer + 1) // 2
+    mirrored = jnp.where(high, outer - 1 - row, row)
+
+    def target_of(step):
+        if step == outer - 1:
+            return row
+        guess = outer - 1 - step
+        guess = jnp.where(guess <= mirrored, guess - 1, guess)
+        return jnp.where(high, outer - 1 - guess, guess)
+
+    def piece(item, part):
+        rows = ins[item].shape[1] // parts
+        return pl.ds(part * rows, rows), part * rows, rows
+
+    def near_hop(item, part, goal):
+        where = piece(item, part)[0]
+        return remote(
+            ins[item].at[goal * inner + 1 - col, where],
+            near[item].at[goal, where],
+            near_send.at[item, part, goal],
+            near_recv.at[item, part, goal],
+            {axis: partner},
+        )
+
+    def far_hop(item, part, goal, landing, sems, peer):
+        where = piece(item, part)[0]
+        return remote(
+            held[item].at[goal, where],
+            landing[item].at[goal, where],
+            far_send.at[item, part, goal],
+            sems.at[item, part, goal],
+            {axis: peer},
+        )
+
+    for step in range(outer):
+        goal = target_of(step)
+        for item in range(items):
+            for part in range(parts):
+                near_hop(item, part, goal).start()
+    for step in range(outer - 1):
+        goal = target_of(step)
+        going_up = goal > row
+        going_down = goal < row
+        for item in range(items):
+            for part in range(parts):
+                where, start, rows = piece(item, part)
+                near_hop(item, part, goal).wait_recv()
+                add_rows(
+                    held[item].at[goal],
+                    ins[item].at[goal * inner + col],
+                    near[item].at[goal],
+                    start,
+                    rows,
+                )
+
+                @pl.when(jnp.logical_and(going_up, row > 0))
+                def _():
+                    far_hop(item, part, goal, above, up_recv, me).wait_recv()
+                    add_rows(held[item].at[goal], held[item].at[goal], above[item].at[goal], start, rows)
+
+                @pl.when(jnp.logical_and(going_down, row < outer - 1))
+                def _():
+                    far_hop(item, part, goal, below, down_recv, me).wait_recv()
+                    add_rows(held[item].at[goal], held[item].at[goal], below[item].at[goal], start, rows)
+
+                @pl.when(going_up)
+                def _():
+                    far_hop(item, part, goal, above, up_recv, links[0][1]).start()
+
+                @pl.when(going_down)
+                def _():
+                    far_hop(item, part, goal, below, down_recv, links[1][1]).start()
+
+    for item in range(items):
+        for part in range(parts):
+            where, start, rows = piece(item, part)
+            near_hop(item, part, row).wait_recv()
+            add_rows(outs[item], ins[item].at[me], near[item].at[row], start, rows)
+
+            @pl.when(row > 0)
+            def _():
+                far_hop(item, part, row, above, up_recv, me).wait_recv()
+                add_rows(outs[item], outs[item], above[item].at[row], start, rows)
+
+            @pl.when(row < outer - 1)
+            def _():
+                far_hop(item, part, row, below, down_recv, me).wait_recv()
+                add_rows(outs[item], outs[item], below[item].at[row], start, rows)
+
+    for step in range(outer):
+        goal = target_of(step)
+        for item in range(items):
+            for part in range(parts):
+                near_hop(item, part, goal).wait_send()
+                if step < outer - 1:
+                    far_hop(item, part, goal, above, up_recv, me).wait_send()
+
+
+def reduce_to_owner(axis, outer, call_id, items, parts, out_dtype):
+    count = len(items)
+    shapes = [item.shape for item in items]
+    buffers = [pltpu.VMEM((outer,) + shape[1:], jnp.bfloat16) for shape in shapes]
+    return pl.pallas_call(
+        functools.partial(reduce_kernel, axis, outer, count, parts),
+        out_shape=[jax.ShapeDtypeStruct(shape[1:], out_dtype) for shape in shapes],
+        in_specs=[VMEM_SPEC] * count,
+        out_specs=[VMEM_SPEC] * count,
+        scratch_shapes=buffers * 4
+        + [
+            pltpu.SemaphoreType.DMA((count, parts, outer)),
+            pltpu.SemaphoreType.DMA((count, parts, outer)),
+            pltpu.SemaphoreType.DMA((count, parts, outer)),
+            pltpu.SemaphoreType.DMA((count, parts, outer)),
+            pltpu.SemaphoreType.DMA((count, parts, outer)),
+        ],
+        compiler_params=comm_params(call_id),
+        name=f"reduce_{call_id}",
+    )(*items)
+
+
+def everyone_kernel(devices, group, summing, in_ref, out_ref, held, send, recv):
+    me = lax.axis_index("dp") * group + lax.axis_index("expert")
+    barrier = pltpu.get_barrier_semaphore()
+
+    def place(step):
+        peer = lax.rem(me + step, devices)
+        return peer, {"dp": peer // group, "expert": lax.rem(peer, group)}
+
+    def greet(step, carry):
+        pl.semaphore_signal(barrier, inc=1, device_id=place(step)[1], device_id_type=MESH)
+        return carry
+
+    lax.fori_loop(1, devices, greet, 0)
+    pl.semaphore_wait(barrier, devices - 1)
+
+    def hop(step):
+        peer, device = place(step)
+        src = in_ref.at[peer] if summing else in_ref
+        return remote(src, held.at[me], send.at[step], recv.at[me], device)
+
+    def begin(step, carry):
+        hop(step).start()
+        return carry
+
+    lax.fori_loop(1, devices, begin, 0)
+
+    def finish(step, carry):
+        peer = place(step)[0]
+        src = in_ref.at[peer] if summing else in_ref
+        remote(src, held.at[peer], send.at[step], recv.at[peer], place(step)[1]).wait()
+        return carry
+
+    lax.fori_loop(1, devices, finish, 0)
+    held[me] = in_ref[me] if summing else in_ref[...]
+    if summing:
+        out_ref[...] = lax.fori_loop(
+            1, devices, lambda index, total: total + held[index], held[0]
+        )
+    else:
+        out_ref[...] = held[...]
+
+
+def everyone(block, devices, group, call_id, summing):
+    shape = block.shape[1:] if summing else block.shape
+    return pl.pallas_call(
+        functools.partial(everyone_kernel, devices, group, summing),
+        out_shape=jax.ShapeDtypeStruct(shape if summing else (devices,) + shape, block.dtype),
+        in_specs=[VMEM_SPEC],
+        out_specs=VMEM_SPEC,
+        scratch_shapes=[
+            pltpu.VMEM((devices,) + shape, block.dtype),
+            pltpu.SemaphoreType.DMA((devices,)),
+            pltpu.SemaphoreType.DMA((devices,)),
+        ],
+        compiler_params=comm_params(call_id),
+        name=f"everyone_{call_id}",
+    )(block)
 
 
 def per_device(
@@ -93,52 +485,89 @@
 
     ff_own = replicas * ff_share
 
-    def spread(rows_low):
-        return lax.all_gather(rows_low, "expert", axis=0, tiled=True)
-
-    def fold(partial_sums):
-        return lax.psum_scatter(
-            partial_sums.astype(jnp.bfloat16), "expert", scatter_dimension=0, tiled=True
-        ).astype(jnp.float32)
-
-    def swap(blocks):
-        return lax.all_to_all(blocks, "expert", split_axis=0, concat_axis=0, tiled=True)
-
-    def gather_dp(rows):
-        return lax.all_gather(rows, "dp", axis=0, tiled=True)
-
-    def scatter_dp(rows):
-        return lax.psum_scatter(
-            rows.astype(jnp.bfloat16), "dp", scatter_dimension=0, tiled=True
-        )
-
-    small = lax.all_gather(
-        jnp.concatenate([norm1_gain[:, None], norm2_gain[:, None], w_router, w_mix], axis=1),
-        ("dp", "expert"),
-        axis=0,
-        tiled=True,
-    )
-    gain_one = small[:, 0].astype(jnp.float32)
-    gain_two = small[:, 1].astype(jnp.float32)
-    router_w = small[:, 2 : 2 + experts]
-    mix_w = small[:, 2 + experts :]
-
-    qkv_out = jnp.moveaxis(w_qkv.reshape(row_share, 3, experts, cut_width), 2, 0)
-    qkv_w = gather_dp(swap(qkv_out).reshape(experts * row_share, 3 * cut_width))
-    out_rows = gather_dp(w_out)
-    out_in = swap(out_rows.reshape(experts, stride * row_share, model_width))
+    paired = experts == 4 and replicas == 8
+    devices = replicas * experts
+
+    def expert_exchange(call_id, gathers=(), swaps=()):
+        if paired:
+            outs = exchange("expert", 2, call_id, gathers, swaps)
+            merged = [out.reshape((-1,) + out.shape[2:]) for out in outs[: len(gathers)]]
+            return merged + list(outs[len(gathers) :])
+        return [lax.all_gather(rows, "expert", axis=0, tiled=True) for rows in gathers] + [
+            lax.all_to_all(blocks, "expert", split_axis=0, concat_axis=0, tiled=True)
+            for blocks in swaps
+        ]
+
+    def gather_dp(call_id, arrays):
+        if paired:
+            outs = exchange("dp", 4, call_id, arrays)
+            return [out.reshape((-1,) + out.shape[2:]) for out in outs]
+        return [lax.all_gather(rows, "dp", axis=0, tiled=True) for rows in arrays]
+
+    def scatter(axis, call_id, arrays, parts, out_dtype):
+        lows = [rows.astype(jnp.bfloat16) for rows in arrays]
+        if paired:
+            count = lax.axis_size(axis)
+            return reduce_to_owner(
+                axis,
+                count // 2,
+                call_id,
+                [rows.reshape(count, rows.shape[0] // count, rows.shape[1]) for rows in lows],
+                parts,
+                out_dtype,
+            )
+        return [
+            lax.psum_scatter(rows, axis, scatter_dimension=0, tiled=True).astype(out_dtype)
+            for rows in lows
+        ]
+
+    def fold(call_id, partial_sums):
+        return scatter("expert", call_id, [partial_sums], 2, jnp.float32)[0]
+
+    kinds = jnp.concatenate(
+        [norm1_gain[None], norm2_gain[None], jnp.transpose(w_router), jnp.transpose(w_mix)], axis=0
+    )
+    kind_count = kinds.shape[0]
+    if paired:
+        padded = jnp.pad(kinds, ((0, 16 - kind_count), (0, 128 - row_share)))
+        small = everyone(padded, devices, experts, 0, False)[:, :kind_count, :row_share]
+        small = jnp.transpose(small, (1, 0, 2)).reshape(kind_count, model_width)
+    else:
+        small = lax.all_gather(kinds, ("dp", "expert"), axis=1, tiled=True)
+    gain_one = small[0].astype(jnp.float32)
+    gain_two = small[1].astype(jnp.float32)
+    router_w = jnp.transpose(small[2 : 2 + experts])
+    mix_w = jnp.transpose(small[2 + experts :])
+
+    qkv_out = jnp.moveaxis(w_qkv.reshape(row_share, 3, experts, cut_width), 2, 0).reshape(
+        experts, row_share, 3 * cut_width
+    )
+    up_out = jnp.moveaxis(w_up.reshape(row_share, replicas, experts, ff_share), 2, 0).reshape(
+        experts, row_share, ff_own
+    )
+    qkv_in, up_in = expert_exchange(1, swaps=(qkv_out, up_out))
+    qkv_w, out_rows, up_w, down_w = gather_dp(
+        2,
+        [
+            qkv_in.reshape(experts * row_share, 3 * cut_width),
+            w_out,
+            up_in.reshape(experts * row_share, ff_own),
+            w_down,
+        ],
+    )
+    expert_in_w = expert_up[:, 0, :]
+    expert_out_w = expert_down[:, 0, :]
+
+    inputs = tokens.astype(jnp.float32)
+    scaled_one, normed_one, inverse_one = layer_norm(inputs, gain_one)
+    normed_all, out_in = expert_exchange(
+        3,
+        gathers=(scaled_one.astype(jnp.bfloat16),),
+        swaps=(out_rows.reshape(experts, stride * row_share, model_width),),
+    )
     out_w = jnp.transpose(
         out_in.reshape(experts, stride, row_share, model_width), (1, 0, 2, 3)
     ).reshape(cut_width, model_width)
-    up_out = jnp.moveaxis(w_up.reshape(row_share, replicas, experts, ff_share), 2, 0)
-    up_w = gather_dp(swap(up_out).reshape(experts * row_share, ff_own))
-    down_w = gather_dp(w_down)
-    expert_in_w = expert_up[:, 0, :]
-    expert_out_w = expert_down[:, 0, :]
-
-    inputs = tokens.astype(jnp.float32)
-    scaled_one, normed_one, inverse_one = layer_norm(inputs, gain_one)
-    normed_all = spread(scaled_one.astype(jnp.bfloat16))
     seq_len = normed_all.shape[0]
     qkv_cut = jnp.dot(normed_all, qkv_w, preferred_element_type=jnp.float32).astype(jnp.bfloat16)
     queries = qkv_cut[:, :cut_width].reshape(seq_len, head_count, HEAD)
@@ -161,7 +590,7 @@
         .reshape(seq_len, cut_width)
         .astype(jnp.bfloat16)
     )
-    attn_out = fold(jnp.dot(attended_cut, out_w, preferred_element_type=jnp.float32))
+    attn_out = fold(4, jnp.dot(attended_cut, out_w, preferred_element_type=jnp.float32))
     middle = inputs + attn_out
     scaled_two, normed_two, inverse_two = layer_norm(middle, gain_two)
     hidden_low = scaled_two.astype(jnp.bfloat16)
@@ -191,11 +620,14 @@
     send_rows = contract_rows(picks, jnp.concatenate([hidden_low, grad_expert], axis=1)).astype(
         jnp.bfloat16
     )
-    received = swap(send_rows.reshape(experts, capacity, 2 * model_width))
-    routed = gather_dp(received.reshape(slot_rows, 2 * model_width))
+    dense_rows, received = expert_exchange(
+        5,
+        gathers=(jnp.concatenate([hidden_low, grad_dense], axis=1),),
+        swaps=(send_rows.reshape(experts, capacity, 2 * model_width),),
+    )
+    routed = gather_dp(6, [received.reshape(slot_rows, 2 * model_width)])[0]
     routed_in = routed[:, :model_width]
     routed_grad = routed[:, model_width:]
-    dense_rows = spread(jnp.concatenate([hidden_low, grad_dense], axis=1))
     hidden_all = dense_rows[:, :model_width]
     grad_dense_all = dense_rows[:, model_width:]
 
@@ -210,7 +642,7 @@
         ],
         axis=1,
     )
-    dense_back = fold(dense_sums)
+    dense_back = fold(7, dense_sums)
     dense_out = dense_back[:, :model_width]
     grad_w_down_cut = contract_rows(dense_act, grad_dense_all)
     grad_w_up_cut = contract_rows(hidden_all, grad_pre_d)
@@ -232,7 +664,10 @@
     )
     grad_expert_up = contract_rows(grad_pre_e, routed_in)
     grad_expert_down = contract_rows(act_low, routed_grad)
-    expert_back = swap(scatter_dp(expert_sums).reshape(experts, capacity, 2 * model_width))
+    expert_sum = scatter("dp", 8, [expert_sums], 4, jnp.bfloat16)[0]
+    expert_back = expert_exchange(
+        9, swaps=(expert_sum.reshape(experts, capacity, 2 * model_width),)
+    )[0]
     expert_rows_all = jnp.dot(
         picks, expert_back.reshape(slot_rows, 2 * model_width), preferred_element_type=jnp.float32
     )
@@ -266,7 +701,7 @@
     grad_w_mix = precise_rows(grad_mix, hidden_wide)
     grad_mid_norm, grad_gain_two = norm_back(grad_hidden, normed_two, inverse_two, gain_two)
     grad_middle = grad_out + grad_mid_norm
-    grad_attn_all = spread(grad_middle.astype(jnp.bfloat16))
+    grad_attn_all = expert_exchange(10, gathers=(grad_middle.astype(jnp.bfloat16),))[0]
     grad_w_out_cut = contract_rows(attended_cut, grad_attn_all)
     grad_att_cut = (
         contract_cols(grad_attn_all, out_w)
@@ -299,41 +734,57 @@
         axis=1,
     ).astype(jnp.bfloat16)
     grad_w_qkv_cut = contract_rows(normed_all, grad_qkv_cut)
-    grad_normed = fold(contract_cols(grad_qkv_cut, qkv_w))
+    grad_normed = fold(11, contract_cols(grad_qkv_cut, qkv_w))
     grad_in_norm, grad_gain_one = norm_back(grad_normed, normed_one, inverse_one, gain_one)
     grad_tokens = grad_middle + grad_in_norm
 
-    up_sum = swap(
-        scatter_dp(grad_w_up_cut).reshape(experts, row_share, replicas, ff_share)
-    )
-    grad_w_up = (
-        jnp.transpose(up_sum, (1, 2, 0, 3)).reshape(row_share, experts * ff_own)
-    ).astype(jnp.float32)
-    grad_w_down = scatter_dp(grad_w_down_cut).astype(jnp.float32)
     out_send = jnp.transpose(
         grad_w_out_cut.astype(jnp.bfloat16).reshape(stride, experts, row_share, model_width),
         (1, 0, 2, 3),
-    )
-    grad_w_out = scatter_dp(swap(out_send).reshape(replicas * row_share, model_width)).astype(
-        jnp.float32
-    )
-    qkv_sum = swap(scatter_dp(grad_w_qkv_cut).reshape(experts, row_share, 3, cut_width))
+    ).reshape(experts, stride * row_share, model_width)
+    out_mine = expert_exchange(12, swaps=(out_send,))[0].reshape(
+        replicas * row_share, model_width
+    )
+    grad_w_down, up_sum, grad_w_out, qkv_sum = scatter(
+        "dp", 13, [grad_w_down_cut, grad_w_up_cut, out_mine, grad_w_qkv_cut], 1, jnp.float32
+    )
+    up_back, qkv_back = expert_exchange(
+        14,
+        swaps=(
+            up_sum.astype(jnp.bfloat16).reshape(experts, row_share, ff_own),
+            qkv_sum.astype(jnp.bfloat16).reshape(experts, row_share, 3 * cut_width),
+        ),
+    )
+    grad_w_up = (
+        jnp.transpose(up_back.reshape(experts, row_share, replicas, ff_share), (1, 2, 0, 3))
+        .reshape(row_share, experts * ff_own)
+        .astype(jnp.float32)
+    )
     grad_w_qkv = (
-        jnp.transpose(qkv_sum, (1, 2, 0, 3)).reshape(row_share, 3 * model_width)
-    ).astype(jnp.float32)
-
-    totals = lax.psum(
-        (
-            jnp.concatenate(
-                [grad_gain_one[None], grad_gain_two[None], grad_w_router, grad_w_mix], axis=0
-            ),
-            square_stats,
-        ),
-        ("dp", "expert"),
-    )
-    own = lax.dynamic_slice_in_dim(totals[0], my_block * row_share, row_share, 1)
+        jnp.transpose(qkv_back.reshape(experts, row_share, 3, cut_width), (1, 2, 0, 3))
+        .reshape(row_share, 3 * model_width)
+        .astype(jnp.float32)
+    )
+
+    kind_grads = jnp.concatenate(
+        [grad_gain_one[None], grad_gain_two[None], grad_w_router, grad_w_mix], axis=0
+    )
+    if paired:
+        slices = jnp.transpose(kind_grads.reshape(kind_count, devices, row_share), (1, 0, 2))
+        slices = jnp.pad(slices, ((0, 0), (0, 0), (0, 128 - row_share)))
+        stats = jnp.broadcast_to(
+            jnp.pad(square_stats[None, None], ((0, 0), (0, 7), (0, 124))), (devices, 8, 128)
+        )
+        owned = everyone(
+            jnp.concatenate([slices, stats], axis=1), devices, experts, 15, True
+        )
+        own = owned[:kind_count, :row_share]
+        square_sums = owned[kind_count, :4]
+    else:
+        totals, square_sums = lax.psum((kind_grads, square_stats), ("dp", "expert"))
+        own = lax.dynamic_slice_in_dim(totals, my_block * row_share, row_share, 1)
     entry_count = local_rows * model_width * replicas * experts
-    rms_values = jnp.sqrt(totals[1] / entry_count + 1e-06)
+    rms_values = jnp.sqrt(square_sums / entry_count + 1e-06)
     return (
         result,
         grad_tokens,

time: 958 us -> 654 us (0.68)
  waiting for transfers between devices: 627 us -> 0 us
  Pallas kernels: 0 us -> 506 us
  blocking collectives: 153 us -> 0 us
  starting transfers between devices: 18.8 us -> 0 us
  between operations: 15.6 us -> 2.74 us
  local copies, waits for them, and re-layouts: 25.2 us -> 37.4 us
  matrix products: 78 us -> 68.1 us
    pallas_call x0 -> x16, Pallas kernels: none -> 506 us  [the longest x9 268 us: exchange(): pl.pallas_call(functools.partial(exchange_kernel, axis, outer, inner, len...]
    reduce_scatter x8 -> x0, waiting for transfers between devices: 395 us -> none  [the longest x5 320 us: scatter_dp(): lax.psum_scatter(rows.astype(jnp.bfloat16), 'dp', scatter_dimension=0, ti...]
    all_gather x7 -> x0, waiting for transfers between devices: 216 us -> none  [the longest x4 185 us: gather_dp(): return lax.all_gather(rows, 'dp', axis=0, tiled=True)]
    all_gather x2 -> x0, blocking collectives: 77.2 us -> none  [the longest x1 43.4 us: per_device(): lax.all_gather(jnp.concatenate([norm1_gain[:, None], norm2_gain[:, None],...]
    psum x1 -> x0, blocking collectives: 39.9 us -> none  [per_device(): lax.psum((jnp.concatenate([grad_gain_one[None], grad_gain_two[None], grad...]
    all_to_all x3 -> x0, blocking collectives: 36.1 us -> none  [swap(): lax.all_to_all(blocks, 'expert', split_axis=0, concat_axis=0, tiled=True)]
    all_to_all x5 -> x0, starting transfers between devices: 17.4 us -> none  [swap(): lax.all_to_all(blocks, 'expert', split_axis=0, concat_axis=0, tiled=True)]
    all_to_all x5 -> x0, waiting for transfers between devices: 14.6 us -> none  [swap(): lax.all_to_all(blocks, 'expert', split_axis=0, concat_axis=0, tiled=True)]
  transfers between devices with their start and end apart: 20 -> 0, of which waited for: 17 -> 0; matrix products, arithmetic and copies ran while one was open for 11% -> 0% of each run, Pallas kernels for 0% -> 0%
where the time goes in v2:
time: 654 us; the launch traced here: 647 us
  Pallas kernels  506 us (77%)
  matrix products  68.1 us (10%)
  local copies, waits for them, and re-layouts  37.4 us (6%)
  other arithmetic  32.5 us (5%)
    pallas_call x9, Pallas kernels, exchange(): pl.pallas_call(functools.partial(exchange_kernel, axis, outer, inner, len...  268 us
    pallas_call x5, Pallas kernels, reduce_to_owner(): pl.pallas_call(functools.partial(reduce_kernel, axis, outer, count, parts...  216 us
    pallas_call x2, Pallas kernels, everyone(): pl.pallas_call(functools.partial(everyone_kernel, devices, group, summing...  22.8 us
    dot_general x6, matrix products, contract_cols(): lax.dot_general(left_side, right_side, COLS_AXIS, preferred_element_type=...  17.6 us
    dot_general x7, matrix products, contract_rows(): lax.dot_general(left_side, right_side, ROWS_AXIS, preferred_element_type=...  16.5 us

profile of v2, /device:TPU:0, one launch (start us, length us, event | category | flops | bytes accessed | tf_op | source)
XLA Modules:
  0.0 646.7 jit_solution(8261843998555229069)
XLA Ops:
  6.6 12.0 %everyone_0.1 = bf16[32,16,128]{2,1,0:T(8,128)(2,1)} custom-call(bf16[16,128]{1,0:T(8,128)(2,1)} %fusion.86.in_ref), custom_call_target="tpu_custom_call" | custom-call | tf_op jit(solution)/shard_map/everyone_0/pallas_call | solution.py:442
  24.1 8.8 %exchange_1.1 = (bf16[4,32,768]{2,1,0:T(8,128)(2,1)}, bf16[4,32,1024]{2,1,0:T(8,128)(2,1)}) custom-call(bf16[4,32,768]{2,1,0:T(8,128)(2,1)} %reshape.305.refs_0_, bf16[4,32,1024]{2,1,0:T(8,128)(2,1)} %reshape.307.refs_1_), custom_call_target="tpu_custom_call" | custom-call | tf_op jit(solution)/shard_map/exchange_1/pallas_call | solution.py:226
  32.9 79.1 %exchange_2.1 = (bf16[8,128,768]{2,1,0:T(8,128)(2,1)}, bf16[8,32,1024]{2,1,0:T(8,128)(2,1)}, bf16[8,128,1024]{2,1,0:T(8,128)(2,1)}, bf16[8,128,1024]{2,1,0:T(8,128)(2,1)}) custom-call(bf16[128,768]{1,0:T(8,128)(2,1)} %bitcast.220, bf16[32,1024]{1,0:T(8,128)(2,1)} %refs_1_.1, bf16[128,1024]{1,0:T(8,128)(2,1)} %bitcast.212, bf16[128,1024]{1,0:T(8,128)(2,1)} %refs_3_.1), custom_call_target="tpu_custom_call" | custom-call | tf_op jit(solution)/shard_map/exchange_2/pallas_call | solution.py:226
  112.1 14.7 %exchange_3.1 = (bf16[4,128,1024]{2,1,0:T(8,128)(2,1)}, bf16[4,64,1024]{2,1,0:T(8,128)(2,1)}) custom-call(bf16[128,1024]{1,0:T(8,128)(2,1)} %fusion.59.refs_0_, bf16[4,64,1024]{2,1,0:T(8,128)(2,1)} %bitcast.210), custom_call_target="tpu_custom_call" | custom-call | tf_op jit(solution)/shard_map/exchange_3/pallas_call | solution.py:226
  131.2 3.6 fusion.117
  138.9 13.1 %reduce_4.1 = f32[128,1024]{1,0:T(8,128)} custom-call(bf16[4,128,1024]{2,1,0:T(8,128)(2,1)} %bitcast.185), custom_call_target="tpu_custom_call" | custom-call | tf_op jit(solution)/shard_map/reduce_4/pallas_call | solution.py:380
  157.3 25.1 %exchange_5.1 = (bf16[4,128,2048]{2,1,0:T(8,128)(2,1)}, bf16[4,64,2048]{2,1,0:T(8,128)(2,1)}) custom-call(bf16[128,2048]{1,0:T(8,128)(2,1)} %pad_maximum_fusion.4.refs_0_, bf16[4,64,2048]{2,1,0:T(8,128)(2,1)} %bitcast.187), custom_call_target="tpu_custom_call" | custom-call | tf_op jit(solution)/shard_map/exchange_5/pallas_call | solution.py:226
  192.9 18.9 %reduce_7.1 = f32[128,2048]{1,0:T(8,128)} custom-call(bf16[4,128,2048]{2,1,0:T(8,128)(2,1)} %bitcast.181), custom_call_target="tpu_custom_call" | custom-call | tf_op jit(solution)/shard_map/reduce_7/pallas_call | solution.py:380
  211.9 4.8 convolution_convert_fusion.4
  219.3 93.1 %exchange_6.1 = bf16[8,256,2048]{2,1,0:T(8,128)(2,1)} custom-call(bf16[256,2048]{1,0:T(8,128)(2,1)} %bitcast.198), custom_call_target="tpu_custom_call" | custom-call | tf_op jit(solution)/shard_map/exchange_6/pallas_call | solution.py:226
  312.4 5.1 fusion.14
  317.5 5.0 fusion.7
  327.4 4.4 convolution_convert_fusion.1
  338.8 4.4 convolution_convert_fusion
  343.2 8.4 %pad_maximum_fusion = bf16[2048,2048]{0,1:T(8,128)(2,1)} fusion(bf16[2048,1024]{0,1:T(8,128)(2,1)} %convolution_convert_fusion, bf16[2048,1024]{0,1:T(8,128)(2,1)} %convolution_convert_fusion.1), kind=kLoop, calls=%fused_computation.1 | loop fusion | flops 16777216 | bytes 16777216 | tf_op jit(solution)/shard_map/concatenate | solution.py:654
  351.6 12.3 %copy.76 = bf16[2048,2048]{1,0:T(8,128)(2,1)} copy(bf16[2048,2048]{0,1:T(8,128)(2,1)} %pad_maximum_fusion) | data formatting | bytes 16777216 | tf_op jit(solution)/shard_map/concatenate | solution.py:654
  363.9 95.8 %reduce_8.1 = bf16[256,2048]{1,0:T(8,128)(2,1)} custom-call(bf16[8,256,2048]{2,1,0:T(8,128)(2,1)} %bitcast.176), custom_call_target="tpu_custom_call" | custom-call | tf_op jit(solution)/shard_map/reduce_8/pallas_call | solution.py:380
  459.7 17.4 %exchange_9.1 = bf16[4,64,2048]{2,1,0:T(8,128)(2,1)} custom-call(bf16[4,64,2048]{2,1,0:T(8,128)(2,1)} %bitcast.184), custom_call_target="tpu_custom_call" | custom-call | tf_op jit(solution)/shard_map/exchange_9/pallas_call | solution.py:226
  486.5 11.8 %exchange_10.1 = bf16[4,128,1024]{2,1,0:T(8,128)(2,1)} custom-call(bf16[128,1024]{1,0:T(8,128)(2,1)} %get-tuple-element.110.refs_0_), custom_call_target="tpu_custom_call" | custom-call | tf_op jit(solution)/shard_map/exchange_10/pallas_call | solution.py:226
  501.4 8.1 %exchange_12.1 = bf16[4,64,1024]{2,1,0:T(8,128)(2,1)} custom-call(bf16[4,64,1024]{2,1,0:T(8,128)(2,1)} %bitcast.195), custom_call_target="tpu_custom_call" | custom-call | tf_op jit(solution)/shard_map/exchange_12/pallas_call | solution.py:226
  520.8 75.2 %reduce_13.1 = (f32[128,1024]{1,0:T(8,128)}, f32[128,1024]{1,0:T(8,128)}, f32[32,1024]{1,0:T(8,128)}, f32[128,768]{1,0:T(8,128)}) custom-call(bf16[8,128,1024]{2,1,0:T(8,128)(2,1)} %bitcast.188, bf16[8,128,1024]{2,1,0:T(8,128)(2,1)} %bitcast.189, bf16[8,32,1024]{2,1,0:T(8,128)(2,1)} %bitcast.192, bf16[8,128,768]{2,1,0:T(8,128)(2,1)} %bitcast.197), custom_call_target="tpu_custom_call" | custom-call | tf_op jit(solution)/shard_map/reduce_13/pallas_call | solution.py:380
  597.7 12.6 %reduce_11.1 = f32[128,1024]{1,0:T(8,128)} custom-call(bf16[4,128,1024]{2,1,0:T(8,128)(2,1)} %bitcast.207), custom_call_target="tpu_custom_call" | custom-call | tf_op jit(solution)/shard_map/reduce_11/pallas_call | solution.py:380
  614.7 10.9 %everyone_15.1 = f32[16,128]{1,0:T(8,128)} custom-call(f32[32,16,128]{2,1,0:T(8,128)} %select_maximum_fusion.in_ref), custom_call_target="tpu_custom_call" | custom-call | tf_op jit(solution)/shard_map/everyone_15/pallas_call | solution.py:442
  631.3 9.4 %exchange_14.1 = (bf16[4,32,1024]{2,1,0:T(8,128)(2,1)}, bf16[4,32,768]{2,1,0:T(8,128)(2,1)}) custom-call(bf16[4,32,1024]{2,1,0:T(8,128)(2,1)} %bitcast.201, bf16[4,32,768]{2,1,0:T(8,128)(2,1)} %bitcast.209), custom_call_target="tpu_custom_call" | custom-call | tf_op jit(solution)/shard_map/exchange_14/pallas_call | solution.py:226
  (174 shorter events, 90.0 us)
Async XLA Ops:
  0.6 316.8 %copy-start = (bf16[512,1,1024]{2,0,1:T(8,128)(2,1)S(1)}, bf16[512,1,1024]{2,0,1:T(8,128)(2,1)}, u32[]{:S(2)}) copy-start(bf16[512,1,1024]{2,0,1:T(8,128)(2,1)} %param.27) | copy-start | bytes 3145732
  0.7 21.5 %copy-start.2 = (bf16[128,1024]{1,0:T(8,128)(2,1)S(1)}, bf16[128,1024]{1,0:T(8,128)(2,1)}, u32[]{:S(2)}) copy-start(bf16[128,1024]{1,0:T(8,128)(2,1)} %param.14) | copy-start | bytes 786436
  0.7 22.4 %copy-start.16 = (bf16[32,4096]{1,0:T(8,128)(2,1)S(1)}, bf16[32,4096]{1,0:T(8,128)(2,1)}, u32[]{:S(2)}) copy-start(bf16[32,4096]{1,0:T(8,128)(2,1)} %param.22) | copy-start | bytes 786436
  130.8 3.9 copy-start.10
  131.0 3.8 copy-start.12
  131.2 3.6 copy-start.17
  138.9 15.8 %copy-start.21 = (s32[128,1]{0,1:T(1,128)S(1)}, s32[128,1]{0,1:T(1,128)}, u32[]{:S(2)}) copy-start(s32[128,1]{0,1:T(1,128)} %param.17) | copy-start | bytes 1540
  138.9 15.8 %copy-start.7 = (bf16[128,1024]{1,0:T(8,128)(2,1)S(1)}, bf16[128,1024]{1,0:T(8,128)(2,1)}, u32[]{:S(2)}) copy-start(bf16[128,1024]{1,0:T(8,128)(2,1)} %param.15) | copy-start | bytes 786436
  182.4 3.3 copy-start.23
  182.4 3.3 copy-start.24
  185.7 2.4 copy-start.29
  211.8 4.8 copy-start.25
  211.9 4.8 copy-start.31
  312.4 5.1 copy-start.3
  335.3 3.5 copy-start.27
  459.7 19.0 %copy-start.5 = (f32[128,2048]{1,0:T(8,128)S(1)}, f32[128,2048]{1,0:T(8,128)}, u32[]{:S(2)}) copy-start(f32[128,2048]{1,0:T(8,128)} %reduce_7.1) | copy-start | bytes 3145732
  485.7 14.4 %copy-start.9 = (bf16[4,64,512]{2,1,0:T(8,128)(2,1)S(1)}, bf16[4,64,512]{2,1,0:T(8,128)(2,1)}, u32[]{:S(2)}) copy-start(bf16[4,64,512]{2,1,0:T(8,128)(2,1)} %copy-done.8) | copy-start | bytes 786436
  509.5 3.5 copy-start.4
  509.5 3.5 copy-start.18
  610.3 20.3 %copy-start.15 = (f32[128,768]{1,0:T(8,128)S(1)}, f32[128,768]{1,0:T(8,128)}, u32[]{:S(2)}) copy-start(f32[128,768]{1,0:T(8,128)} %get-tuple-element.43) | copy-start | bytes 1179652
  640.8 2.5 copy-start.19
  641.9 2.8 copy-start.20
  642.2 3.1 copy-start.14
  642.3 3.9 copy-start.1
  (8 other events, 12.5 us)
